TPU v7x, 512 devices: a whole 4x8x8 slice. The times are simulated.
512 devices in a mesh: batch: 64 (over x, z, y_hi), space: 8 (over y_lo, core).
Axes of the slice: x: 4, y: 8 (y_hi: 2, y_lo: 4; y = y_hi * 4 + y_lo), z: 8, core: 2. Of those that a mesh axis runs over, the one named last changes fastest.
Arguments:
- latents: float32 [64, 32, 64, 4], P('batch', 'space'), may hold values from -16 to 16
- noise_draw: float32 [64, 32, 64, 4], P('batch', 'space'), may hold values from -5 to 5
- timesteps: int32 [64], P('batch'), may hold values from 200 to 799
- inlet_conv: bfloat16 [36, 320], replicated, may hold values from -1 to 1
- time_first: bfloat16 [320, 1280], P(None, 'batch'), may hold values from -0.3125 to 0.3125
- time_first_bias: float32 [1280], replicated, may hold values from -4 to 4
- time_second: bfloat16 [1280, 320], P(None, 'batch'), may hold values from -0.3125 to 0.3125
- time_second_bias: float32 [320], replicated, may hold values from -4 to 4
- conv_first: bfloat16 [2880, 320], P(None, 'batch'), may hold values from -0.109375 to 0.109375
- conv_second: bfloat16 [2880, 320], P(None, 'batch'), may hold values from -0.109375 to 0.109375
- proj_inner: bfloat16 [320, 320], P(None, 'batch'), may hold values from -0.3125 to 0.3125
- query_weight: bfloat16 [320, 320], P(None, 'batch'), may hold values from -30 to 30
- key_weight: bfloat16 [320, 320], P(None, 'batch'), may hold values from -1 to 1
- value_weight: bfloat16 [320, 320], P(None, 'batch'), may hold values from -0.625 to 0.625
- attn_out: bfloat16 [320, 320], P(None, 'batch'), may hold values from -0.625 to 0.625
- proj_outer: bfloat16 [320, 320], P(None, 'batch'), may hold values from -0.3125 to 0.3125
- outlet_conv: bfloat16 [2880, 4], replicated, may hold values from -0.109375 to 0.109375
- first_gain: float32 [320], replicated, may hold values from 0.1 to 1.9
- second_gain: float32 [320], replicated, may hold values from 0.1 to 1.9
- third_gain: float32 [320], replicated, may hold values from 0.1 to 1.9
- final_gain: float32 [320], replicated, may hold values from 0.1 to 1.9
- layer_gain: float32 [320], replicated, may hold values from 0.1 to 1.9
Outputs:
- guidance: float32 [64, 32, 64, 4], P('batch', 'space')
All inputs are finite; a program needn't handle non-finite values.
Results may differ from a plain program's by a relative error of at most 0.029.
Values may be sent and summed in bfloat16 or wider, within the bound.
A program may use at most 64 MiB of HBM per device.

v0:
```python
import math

import jax
import jax.numpy as jnp
from jax import lax
from jax.sharding import PartitionSpec as P

HEADS = 8
HEAD_SIZE = 40
GROUPS = 32
STEPS = 1000


EPS_GROUP = 1e-06
EPS_BLOCK = 1e-05
EPS_LAYER = 1e-05


def laid_out(parts, dim):
    parts = jnp.moveaxis(parts, 0, dim)
    shape = parts.shape
    return parts.reshape(*shape[:dim], shape[dim] * shape[dim + 1], *shape[dim + 2 :])


def from_everyone(shard, axis):
    length = lax.axis_size(axis)
    return lax.all_to_all(
        jnp.broadcast_to(shard[None], (length, *shard.shape)), axis, 0, 0, tiled=True
    )


def collect(shard, axis, dim):
    return laid_out(from_everyone(shard, axis), dim)


def extended(cells, sides, width):
    for axis, dim in sides:
        count = lax.axis_size(axis)
        ends = count - 1
        head = lax.slice_in_dim(cells, 0, width, axis=dim)
        tail = lax.slice_in_dim(cells, cells.shape[dim] - width, cells.shape[dim], axis=dim)
        cells = jnp.concatenate(
            [
                lax.ppermute(tail, axis, [(i, (i + 1) % count) for i in range(ends)]),
                cells,
                lax.ppermute(head, axis, [((i + 1) % count, i) for i in range(ends)]),
            ],
            axis=dim,
        )
    return cells


def of_everyone(shard, axis):
    everything = from_everyone(shard, axis)
    return jnp.sum(everything, axis=0)


def packed_total(arrays, axis):
    vector, at, gathered = (jnp.concatenate([a.reshape(-1) for a in arrays]), 0, [])
    running = of_everyone(vector, axis)
    for a in arrays:
        gathered.append(running[at : at + a.size].reshape(a.shape))
        at += a.size
    return tuple(gathered)


def in_one_piece(arrays, axis, dim, along):
    widths = [a.shape[along] for a in arrays]
    both = jnp.concatenate(arrays, axis=along)
    filled = lax.all_gather(both, axis, axis=dim, tiled=True)
    return tuple(jnp.split(filled, [sum(widths[:k]) for k in range(1, len(widths))], axis=along))


def turned_gather(arrays, axis, dims):
    turned = [jnp.moveaxis(a, dim, 0) for a, dim in zip(arrays, dims)]
    widths = [t[0].size for t in turned]
    both = jnp.concatenate([t.reshape(-1, w) for t, w in zip(turned, widths)], axis=1)
    filled = lax.all_gather(both, axis, axis=0, tiled=True)
    parts = jnp.split(filled, [sum(widths[:k]) for k in range(1, len(widths))], axis=1)
    return tuple(
        (
            jnp.moveaxis(b.reshape(-1, *t.shape[1:]), 0, dim)
            for b, t, dim in zip(parts, turned, dims)
        )
    )


def plan():
    fraction = jnp.arange(STEPS, dtype=jnp.float32) / (STEPS - 1)
    beta_root = math.sqrt(0.00085) + fraction * (math.sqrt(0.012) - math.sqrt(0.00085))
    return jnp.cumprod(1.0 - beta_root * beta_root)


def lookup(timesteps):
    plan_tab = plan()
    matches = jnp.arange(STEPS, dtype=jnp.int32)[None, :] == timesteps[:, None]
    return jnp.sum(jnp.where(matches, plan_tab[None, :], 0.0), axis=1)


def waveform_of(timesteps, halfway):
    frequency = jnp.exp(-math.log(10000.0) * jnp.arange(halfway, dtype=jnp.float32) / halfway)
    angles = timesteps.astype(jnp.float32)[:, None] * frequency[None, :]
    return jnp.concatenate([jnp.cos(angles), jnp.sin(angles)], axis=1).astype(jnp.bfloat16)


def embed_sharded(timesteps, first, first_bias, second, second_bias):
    all_steps = collect(timesteps, "batch", 0)
    position = lax.axis_index("batch")
    width_one = first.shape[1]
    width_two = second.shape[1]
    waveform = waveform_of(all_steps, first.shape[0] // 2)
    bias_one = lax.dynamic_slice_in_dim(first_bias, position * width_one, width_one, 0)
    inner = jax.nn.silu(jnp.dot(waveform, first, preferred_element_type=jnp.float32) + bias_one)
    hidden = jax.nn.silu(inner).astype(jnp.bfloat16)
    hidden_all = collect(hidden, "batch", 1)
    bias_two = lax.dynamic_slice_in_dim(second_bias, position * width_two, width_two, 0)
    columns = jnp.dot(hidden_all, second, preferred_element_type=jnp.float32) + bias_two
    return lax.all_to_all(columns, "batch", split_axis=0, concat_axis=1, tiled=True)


def convolve(padded, kernel):
    height = padded.shape[1] - 2
    breadth = padded.shape[2] - 2
    width_in = padded.shape[3]
    result = None
    for offset in range(9):
        row_off, col_off = (offset // 3, offset % 3)
        window = padded[:, row_off : row_off + height, col_off : col_off + breadth, :]
        partial_sum = jnp.einsum(
            "bhwc,cd->bhwd",
            window,
            kernel[offset * width_in : (offset + 1) * width_in],
            preferred_element_type=jnp.float32,
        )
        result = partial_sum if result is None else result + partial_sum
    return result


def with_rims(field):
    padded = extended(field, (("space", 1),), 1)
    return jnp.pad(padded, ((0, 0), (0, 0), (1, 1), (0, 0)))


def with_latent_rims(field):
    padded = extended(field, (("space", 1),), 1)
    return jnp.pad(padded, ((0, 0), (0, 0), (1, 1), (0, 0)))


def group_norm(field, gain_vec, epsilon):
    view_n, height, breadth, chan_n = field.shape
    grouped = field.reshape(view_n, height, breadth, GROUPS, chan_n // GROUPS)
    sums_local = jnp.sum(grouped, axis=(1, 2, 4))
    squares_local = jnp.sum(grouped * grouped, axis=(1, 2, 4))
    sums_all, squares_all = packed_total((sums_local, squares_local), "space")
    number = height * lax.axis_size("space") * breadth * (chan_n // GROUPS)
    means = sums_all / number
    squares = squares_all / number
    factor = lax.rsqrt(squares - means * means + epsilon)
    normal_f = (grouped - means[:, None, None, :, None]) * factor[:, None, None, :, None]
    return normal_f.reshape(view_n, height, breadth, chan_n) * gain_vec


def layer_norm(field, gain_vec):
    means = jnp.mean(field, axis=-1, keepdims=True)
    centred = field - means
    spread = jnp.mean(centred * centred, axis=-1, keepdims=True)
    return centred * lax.rsqrt(spread + EPS_LAYER) * gain_vec


def keys_everywhere(queries, key_rows, value_rows):
    view_n, token_n, chan_n = queries.shape
    factor = 1.0 / math.sqrt(HEAD_SIZE)
    query_heads = queries.reshape(view_n, token_n, HEADS, HEAD_SIZE)
    row_max = jnp.full((view_n, HEADS, token_n), -jnp.inf, jnp.float32)
    row_sum = jnp.zeros((view_n, HEADS, token_n), jnp.float32)
    accum = jnp.zeros((view_n, HEADS, token_n, HEAD_SIZE), jnp.float32)
    key_part, value_part = in_one_piece((key_rows, value_rows), "space", 1, 0)
    length = key_part.shape[1]
    block_n = min(512, length)
    for offset in range(0, length, block_n):
        key_blk = key_part[:, offset : offset + block_n]
        value_blk = value_part[:, offset : offset + block_n]
        rows_here = key_blk.shape[1]
        key_blk = key_blk.reshape(view_n, rows_here, HEADS, HEAD_SIZE)
        value_blk = value_blk.reshape(view_n, rows_here, HEADS, HEAD_SIZE)
        scores = (
            jnp.einsum("bqhd,bkhd->bhqk", query_heads, key_blk, preferred_element_type=jnp.float32)
            * factor
        )
        new_max = jnp.maximum(row_max, jnp.max(scores, axis=-1))
        shrink = jnp.exp(row_max - new_max)
        weights = jnp.exp(scores - new_max[..., None])
        row_sum = row_sum * shrink + jnp.sum(weights, axis=-1)
        accum = accum * shrink[..., None] + jnp.einsum(
            "bhqk,bkhd->bhqd",
            weights.astype(jnp.bfloat16),
            value_blk,
            preferred_element_type=jnp.float32,
        )
        row_max = new_max
    row_max, row_sum, accum = (row_max, row_sum, accum)
    result = accum / row_sum[..., None]
    return result.transpose(0, 2, 1, 3).reshape(view_n, token_n, chan_n).astype(jnp.bfloat16)


def project(field, matrix):
    return jnp.einsum("btc,cd->btd", field, matrix, preferred_element_type=jnp.float32)


def body(
    latents,
    noise_draw,
    timesteps,
    inlet_conv,
    time_first,
    time_first_bias,
    time_second,
    time_second_bias,
    conv_first,
    conv_second,
    proj_inner,
    query_weight,
    key_weight,
    value_weight,
    attn_out,
    proj_outer,
    outlet_conv,
    first_gain,
    second_gain,
    third_gain,
    final_gain,
    layer_gain,
):
    gathered = turned_gather(
        (
            conv_first,
            conv_second,
            proj_inner,
            query_weight,
            key_weight,
            value_weight,
            attn_out,
            proj_outer,
        ),
        "batch",
        (1, 1, 1, 1, 1, 1, 1, 1),
    )
    conv_one, conv_two, inner_w, query_w, key_w, value_w, output_w, outer_w = gathered
    embedded = embed_sharded(timesteps, time_first, time_first_bias, time_second, time_second_bias)
    alpha_bar = lookup(timesteps)[:, None, None, None]
    noisy = (jnp.sqrt(alpha_bar) * latents + jnp.sqrt(1.0 - alpha_bar) * noise_draw).astype(
        jnp.bfloat16
    )
    opening = convolve(with_latent_rims(noisy), inlet_conv).astype(jnp.bfloat16)
    active = jax.nn.silu(group_norm(opening.astype(jnp.float32), first_gain, EPS_BLOCK)).astype(
        jnp.bfloat16
    )
    middle = (convolve(with_rims(active), conv_one) + embedded[:, None, None, :]).astype(
        jnp.bfloat16
    )
    active = jax.nn.silu(group_norm(middle.astype(jnp.float32), second_gain, EPS_BLOCK)).astype(
        jnp.bfloat16
    )
    block_one = (opening.astype(jnp.float32) + convolve(with_rims(active), conv_two)).astype(
        jnp.bfloat16
    )
    normed = group_norm(block_one.astype(jnp.float32), third_gain, EPS_GROUP).astype(jnp.bfloat16)
    view_n, height, breadth, chan_n = normed.shape
    flattened = normed.reshape(view_n, height * breadth, chan_n)
    projected = project(flattened, inner_w)
    tokens_in = layer_norm(projected, layer_gain).astype(jnp.bfloat16)
    queries = project(tokens_in, query_w).astype(jnp.bfloat16)
    key_rows = project(tokens_in, key_w).astype(jnp.bfloat16)
    value_rows = project(tokens_in, value_w).astype(jnp.bfloat16)
    attended = keys_everywhere(queries, key_rows, value_rows)
    mixture = (project(attended, output_w) + projected).astype(jnp.bfloat16)
    outer = project(mixture, outer_w).reshape(view_n, height, breadth, chan_n)
    block_two = (block_one.astype(jnp.float32) + outer).astype(jnp.bfloat16)
    active = jax.nn.silu(group_norm(block_two.astype(jnp.float32), final_gain, EPS_BLOCK)).astype(
        jnp.bfloat16
    )
    predicted = convolve(with_rims(active), outlet_conv)
    return (1.0 - alpha_bar) * (predicted - noise_draw)


def solution(mesh):
    in_specs = (
        P("batch", "space", None, None),
        P("batch", "space", None, None),
        P("batch"),
        P(),
        P(None, "batch"),
        P(),
        P(None, "batch"),
        P(),
        P(None, "batch"),
        P(None, "batch"),
        P(None, "batch"),
        P(None, "batch"),
        P(None, "batch"),
        P(None, "batch"),
        P(None, "batch"),
        P(None, "batch"),
        P(),
        P(),
        P(),
        P(),
        P(),
        P(),
    )
    out_specs = P("batch", "space", None, None)
    return jax.shard_map(body, mesh=mesh, in_specs=in_specs, out_specs=out_specs, check_vma=False)
```

profile of v0, /device:TPU:1, one launch (start us, length us, event | category | flops | bytes accessed | tf_op | source)
XLA Modules:
  0.0 351.4 jit_solution(13570895085451096625)
XLA Ops:
  12.2 4.6 %collective-permute-start = (bf16[1,1,64,4]{2,3,1,0:T(4,128)(2,1)S(1)}, bf16[1,1,64,4]{2,3,1,0:T(4,128)(2,1)S(1)}, u32[]{:S(2)}, u32[]{:S(2)}) collective-permute-start(bf16[1,1,64,4]{2,3,1,0:T(4,128)(2,1)S(1)} %get-tuple-element.37), channel_id=1, source_target_pairs={{0,1},{1,2},{2,3},{3,4},{4,5},{5,6},{6,7},{8,9},{9,10},{10,11},{11... | collective-permute-start | bytes 1544 | tf_op jit(solution)/shard_map/ppermute | solution.py:44
  16.8 5.5 %collective-permute-start.1 = (bf16[1,1,64,4]{2,3,1,0:T(4,128)(2,1)S(1)}, bf16[1,1,64,4]{2,3,1,0:T(4,128)(2,1)S(1)}, u32[]{:S(2)}, u32[]{:S(2)}) collective-permute-start(bf16[1,1,64,4]{2,3,1,0:T(4,128)(2,1)S(1)} %get-tuple-element.38), channel_id=1, source_target_pairs={{1,0},{2,1},{3,2},{4,3},{5,4},{6,5},{7,6},{9,8},{10,9},{11,10},{12... | collective-permute-start | bytes 1544 | tf_op jit(solution)/shard_map/ppermute | solution.py:46
  22.8 14.3 %all-to-all-start.1 = ((s32[64,1,1]{2,1,0:T(1,128)}), s32[64,1,1]{2,1,0:T(1,128)S(1)}, u32[]{:S(2)}, u32[]{:S(2)}) async-start(s32[64,1,1]{2,1,0:T(1,128)} %broadcast_in_dim.22), calls=%async_computation.1 | async-start | bytes 65536 | tf_op jit(solution)/shard_map/all_to_all | solution.py:27
  38.7 11.6 %all-to-all-done.1 = s32[64,1,1]{2,1,0:T(1,128)S(1)} async-done(((s32[64,1,1]{2,1,0:T(1,128)}), s32[64,1,1]{2,1,0:T(1,128)S(1)}, u32[]{:S(2)}, u32[]{:S(2)}) %all-to-all-start.1) | async-done | bytes 288 | tf_op jit(solution)/shard_map/all_to_all | solution.py:27
  60.2 5.1 %all-to-all-start = ((f32[8,1,64]{2,1,0:T(1,128)}), f32[8,1,64]{2,1,0:T(1,128)S(1)}, u32[]{:S(2)}, u32[]{:S(2)}) async-start(f32[8,1,64]{2,1,0:T(1,128)} %broadcast_in_dim.21), calls=%async_computation | async-start | bytes 8192 | tf_op jit(solution)/shard_map/all_to_all | solution.py:27
  66.2 3.9 %all-to-all-done = f32[8,1,64]{2,1,0:T(1,128)S(1)} async-done(((f32[8,1,64]{2,1,0:T(1,128)}), f32[8,1,64]{2,1,0:T(1,128)S(1)}, u32[]{:S(2)}, u32[]{:S(2)}) %all-to-all-start) | async-done | bytes 2080 | tf_op jit(solution)/shard_map/all_to_all | solution.py:27
  70.1 4.6 %all-to-all-start.2 = ((bf16[64,2,640]{2,1,0:T(2,128)(2,1)}), bf16[64,2,640]{2,1,0:T(2,128)(2,1)S(1)}, u32[]{:S(2)}, u32[]{:S(2)}) async-start(bf16[64,2,640]{2,1,0:T(2,128)(2,1)} %reshape.912), calls=%async_computation.2 | async-start | bytes 327680 | tf_op jit(solution)/shard_map/all_to_all | solution.py:27
  75.3 2.8 collective-permute-start.2
  80.0 9.5 %all-to-all-done.2 = bf16[64,2,640]{2,1,0:T(2,128)(2,1)S(1)} async-done(((bf16[64,2,640]{2,1,0:T(2,128)(2,1)}), bf16[64,2,640]{2,1,0:T(2,128)(2,1)S(1)}, u32[]{:S(2)}, u32[]{:S(2)}) %all-to-all-start.2) | async-done | bytes 163872 | tf_op jit(solution)/shard_map/all_to_all | solution.py:27
  91.0 6.6 %all-to-all-start.3 = ((f32[64,1,5]{2,1,0:T(1,128)}), f32[64,1,5]{2,1,0:T(1,128)S(1)}, u32[]{:S(2)}, u32[]{:S(2)}) async-start(f32[64,1,5]{2,1,0:T(1,128)} %copy.45), calls=%async_computation.3 | async-start | bytes 65536 | tf_op jit(solution)/shard_map/all_to_all | solution.py:118
  97.8 12.9 %all-to-all-done.3 = f32[64,1,5]{2,1,0:T(1,128)S(1)} async-done(((f32[64,1,5]{2,1,0:T(1,128)}), f32[64,1,5]{2,1,0:T(1,128)S(1)}, u32[]{:S(2)}, u32[]{:S(2)}) %all-to-all-start.3) | async-done | bytes 1312 | tf_op jit(solution)/shard_map/all_to_all | solution.py:118
  112.1 89.3 %all-gather.6.cloned.1.call-done = bf16[64,5,7680]{2,1,0:T(8,128)(2,1)} async-done(((bf16[1,5,7680]{2,1,0:T(8,128)(2,1)}), bf16[64,5,7680]{2,1,0:T(8,128)(2,1)}) %all-gather.6.cloned.1.call-update) | async-done | bytes 4915216 | tf_op jit(solution)/shard_map/all_gather | solution.py:78
  201.4 8.5 %reshape.863 = bf16[320,7680]{1,0:T(8,128)(2,1)} reshape(bf16[64,5,7680]{2,1,0:T(8,128)(2,1)} %all-gather.6.cloned.1.call-done) | data formatting | bytes 9830400
  209.9 4.3 %fusion.187 = (bf16[320,2880]{1,0:T(8,128)(2,1)}, bf16[320,2880]{1,0:T(8,128)(2,1)S(1)}) fusion(bf16[320,7680]{1,0:T(8,128)(2,1)} %reshape.863), kind=kLoop, calls=%fused_computation.299 | loop fusion | bytes 7372800 | tf_op jit(solution)/shard_map/split | solution.py:79
  214.2 4.0 %copy.51 = bf16[320,2880]{0,1:T(8,128)(2,1)} copy(bf16[320,2880]{1,0:T(8,128)(2,1)} %get-tuple-element.20) | data formatting | bytes 3686400
  225.2 13.7 %all_to_all.48 = f32[8,1,64]{2,1,0:T(1,128)S(1)} all-to-all(f32[8,1,64]{2,1,0:T(1,128)S(1)} %broadcast_in_dim.24), channel_id=1, replica_groups=mesh['batch'=64,'space'=8] {'space'}, dimensions={0} | all-to-all | bytes 4096 | tf_op jit(solution)/shard_map/all_to_all | solution.py:27
  239.5 2.8 collective-permute-start.4
  244.4 2.6 copy.52
  254.7 7.6 %all_to_all.49 = f32[8,1,64]{2,1,0:T(1,128)S(1)} all-to-all(f32[8,1,64]{2,1,0:T(1,128)S(1)} %broadcast_in_dim.26), channel_id=1, replica_groups=mesh['batch'=64,'space'=8] {'space'}, dimensions={0} | all-to-all | bytes 4096 | tf_op jit(solution)/shard_map/all_to_all | solution.py:27
  268.7 38.4 %all-gather.4.cloned.1.call-done = bf16[2,2048,320]{1,2,0:T(8,128)(2,1)} async-done(((bf16[2,256,320]{1,2,0:T(8,128)(2,1)}), bf16[2,2048,320]{1,2,0:T(8,128)(2,1)}) %all-gather.4.cloned.1.call-update) | async-done | bytes 2621456 | tf_op jit(solution)/shard_map/all_gather | solution.py:70
  314.5 2.2 fusion.2
  324.7 8.2 %all_to_all.50 = f32[8,1,64]{2,1,0:T(1,128)S(1)} all-to-all(f32[8,1,64]{2,1,0:T(1,128)S(1)} %broadcast_in_dim.28), channel_id=1, replica_groups=mesh['batch'=64,'space'=8] {'space'}, dimensions={0} | all-to-all | bytes 4096 | tf_op jit(solution)/shard_map/all_to_all | solution.py:27
  333.5 2.8 collective-permute-start.6
  338.3 3.5 collective-permute-done.7
  (183 shorter events, 66.2 us)
Async XLA Ops:
  6.5 83.5 %copy-start = (bf16[1280,5]{0,1:T(8,128)(2,1)S(1)}, bf16[1280,5]{0,1:T(8,128)(2,1)}, u32[]{:S(2)}) copy-start(bf16[1280,5]{0,1:T(8,128)(2,1)} %param.28) | copy-start | bytes 38404
  6.5 51.6 %copy-start.3 = (bf16[36,320]{1,0:T(8,128)(2,1)S(1)}, bf16[36,320]{1,0:T(8,128)(2,1)}, u32[]{:S(2)}) copy-start(bf16[36,320]{1,0:T(8,128)(2,1)} %param.25) | copy-start | bytes 69124
  6.5 194.9 %all-gather.6.cloned.1.call-start = ((), (), s32[]{:S(2)}) async-start(), calls=%async_computation.8 | async-start | bytes 7987200 | tf_op jit(solution)/shard_map/all_gather | solution.py:78
  12.2 40.0 %collective-permute-start = (bf16[1,1,64,4]{2,3,1,0:T(4,128)(2,1)S(1)}, bf16[1,1,64,4]{2,3,1,0:T(4,128)(2,1)S(1)}, u32[]{:S(2)}, u32[]{:S(2)}) collective-permute-start(bf16[1,1,64,4]{2,3,1,0:T(4,128)(2,1)S(1)} %get-tuple-element.37), channel_id=1, source_target_pairs={{0,1},{1,2},{2,3},{3,4},{4,5},{5,6},{6,7},{8,9},{9,10},{10,11},{11... | collective-permute-start | bytes 1544 | tf_op jit(solution)/shard_map/ppermute | solution.py:44
  16.8 35.4 %collective-permute-start.1 = (bf16[1,1,64,4]{2,3,1,0:T(4,128)(2,1)S(1)}, bf16[1,1,64,4]{2,3,1,0:T(4,128)(2,1)S(1)}, u32[]{:S(2)}, u32[]{:S(2)}) collective-permute-start(bf16[1,1,64,4]{2,3,1,0:T(4,128)(2,1)S(1)} %get-tuple-element.38), channel_id=1, source_target_pairs={{1,0},{2,1},{3,2},{4,3},{5,4},{6,5},{7,6},{9,8},{10,9},{11,10},{12... | collective-permute-start | bytes 1544 | tf_op jit(solution)/shard_map/ppermute | solution.py:46
  22.8 27.5 %all-to-all-start.1 = ((s32[64,1,1]{2,1,0:T(1,128)}), s32[64,1,1]{2,1,0:T(1,128)S(1)}, u32[]{:S(2)}, u32[]{:S(2)}) async-start(s32[64,1,1]{2,1,0:T(1,128)} %broadcast_in_dim.22), calls=%async_computation.1 | async-start | bytes 65536 | tf_op jit(solution)/shard_map/all_to_all | solution.py:27
  51.2 24.0 %copy-start.5 = (f32[320]{0:T(512)S(1)}, f32[320]{0:T(512)}, u32[]{:S(2)}) copy-start(f32[320]{0:T(512)} %param.39) | copy-start | bytes 3844
  60.2 9.9 %all-to-all-start = ((f32[8,1,64]{2,1,0:T(1,128)}), f32[8,1,64]{2,1,0:T(1,128)S(1)}, u32[]{:S(2)}, u32[]{:S(2)}) async-start(f32[8,1,64]{2,1,0:T(1,128)} %broadcast_in_dim.21), calls=%async_computation | async-start | bytes 8192 | tf_op jit(solution)/shard_map/all_to_all | solution.py:27
  70.1 19.5 %all-to-all-start.2 = ((bf16[64,2,640]{2,1,0:T(2,128)(2,1)}), bf16[64,2,640]{2,1,0:T(2,128)(2,1)S(1)}, u32[]{:S(2)}, u32[]{:S(2)}) async-start(bf16[64,2,640]{2,1,0:T(2,128)(2,1)} %reshape.912), calls=%async_computation.2 | async-start | bytes 327680 | tf_op jit(solution)/shard_map/all_to_all | solution.py:27
  75.3 22.3 %collective-permute-start.2 = (bf16[1,1,64,320]{3,2,1,0:T(8,128)(2,1)S(1)}, bf16[1,1,64,320]{3,2,1,0:T(8,128)(2,1)S(1)}, u32[]{:S(2)}, u32[]{:S(2)}) collective-permute-start(bf16[1,1,64,320]{3,2,1,0:T(8,128)(2,1)S(1)} %get-tuple-element.34), channel_id=1, source_target_pairs={{0,1},{1,2},{2,3},{3,4},{4,5},{5,6},{6,7},{8,9},{9,10},{10,11},{11... | collective-permute-start | bytes 122888 | tf_op jit(solution)/shard_map/ppermute | solution.py:44
  78.1 19.6 %collective-permute-start.3 = (bf16[1,1,64,320]{3,2,1,0:T(8,128)(2,1)S(1)}, bf16[1,1,64,320]{3,2,1,0:T(8,128)(2,1)S(1)}, u32[]{:S(2)}, u32[]{:S(2)}) collective-permute-start(bf16[1,1,64,320]{3,2,1,0:T(8,128)(2,1)S(1)} %get-tuple-element.35), channel_id=1, source_target_pairs={{1,0},{2,1},{3,2},{4,3},{5,4},{6,5},{7,6},{9,8},{10,9},{11,10},{12... | collective-permute-start | bytes 122888 | tf_op jit(solution)/shard_map/ppermute | solution.py:46
  91.0 19.8 %all-to-all-start.3 = ((f32[64,1,5]{2,1,0:T(1,128)}), f32[64,1,5]{2,1,0:T(1,128)S(1)}, u32[]{:S(2)}, u32[]{:S(2)}) async-start(f32[64,1,5]{2,1,0:T(1,128)} %copy.45), calls=%async_computation.3 | async-start | bytes 65536 | tf_op jit(solution)/shard_map/all_to_all | solution.py:118
  97.6 209.5 %all-gather.4.cloned.1.call-start = ((), (), s32[]{:S(2)}) async-start(), calls=%async_computation.7 | async-start | bytes 2949120 | tf_op jit(solution)/shard_map/all_gather | solution.py:70
  223.2 16.1 %copy-start.6 = (f32[320]{0:T(512)S(1)}, f32[320]{0:T(512)}, u32[]{:S(2)}) copy-start(f32[320]{0:T(512)} %param.40) | copy-start | bytes 3844
  239.5 7.5 %collective-permute-start.4 = (bf16[1,1,64,320]{3,2,1,0:T(8,128)(2,1)S(1)}, bf16[1,1,64,320]{3,2,1,0:T(8,128)(2,1)S(1)}, u32[]{:S(2)}, u32[]{:S(2)}) collective-permute-start(bf16[1,1,64,320]{3,2,1,0:T(8,128)(2,1)S(1)} %get-tuple-element.32), channel_id=1, source_target_pairs={{0,1},{1,2},{2,3},{3,4},{4,5},{5,6},{6,7},{8,9},{9,10},{10,11},{11... | collective-permute-start | bytes 122888 | tf_op jit(solution)/shard_map/ppermute | solution.py:44
  242.3 5.4 %collective-permute-start.5 = (bf16[1,1,64,320]{3,2,1,0:T(8,128)(2,1)S(1)}, bf16[1,1,64,320]{3,2,1,0:T(8,128)(2,1)S(1)}, u32[]{:S(2)}, u32[]{:S(2)}) collective-permute-start(bf16[1,1,64,320]{3,2,1,0:T(8,128)(2,1)S(1)} %get-tuple-element.33), channel_id=1, source_target_pairs={{1,0},{2,1},{3,2},{4,3},{5,4},{6,5},{7,6},{9,8},{10,9},{11,10},{12... | collective-permute-start | bytes 122888 | tf_op jit(solution)/shard_map/ppermute | solution.py:46
  247.0 5.6 %copy-start.1 = (bf16[320,2880]{0,1:T(8,128)(2,1)S(1)}, bf16[320,2880]{0,1:T(8,128)(2,1)}, u32[]{:S(2)}) copy-start(bf16[320,2880]{0,1:T(8,128)(2,1)} %copy.52) | copy-start | bytes 5529604
  252.6 10.0 %copy-start.7 = (f32[320]{0:T(512)S(1)}, f32[320]{0:T(512)}, u32[]{:S(2)}) copy-start(f32[320]{0:T(512)} %param.41) | copy-start | bytes 3844
  252.9 11.2 %copy-start.8 = (f32[320]{0:T(512)S(1)}, f32[320]{0:T(512)}, u32[]{:S(2)}) copy-start(f32[320]{0:T(512)} %param.43) | copy-start | bytes 3844
  320.4 13.0 %copy-start.9 = (f32[320]{0:T(512)S(1)}, f32[320]{0:T(512)}, u32[]{:S(2)}) copy-start(f32[320]{0:T(512)} %param.42) | copy-start | bytes 3844
  320.4 21.4 %copy-start.10 = (bf16[2880,4]{0,1:T(4,128)(2,1)S(1)}, bf16[2880,4]{0,1:T(4,128)(2,1)}, u32[]{:S(2)}) copy-start(bf16[2880,4]{0,1:T(4,128)(2,1)} %param.38) | copy-start | bytes 69124
  321.4 22.2 %copy-start.4 = (f32[1,4,64,4]{2,3,1,0:T(4,128)S(1)}, f32[1,4,64,4]{2,3,1,0:T(4,128)}, u32[]{:S(2)}) copy-start(f32[1,4,64,4]{2,3,1,0:T(4,128)} %param.23) | copy-start | bytes 12292
  333.5 4.7 %collective-permute-start.6 = (bf16[1,1,64,320]{3,2,1,0:T(8,128)(2,1)S(1)}, bf16[1,1,64,320]{3,2,1,0:T(8,128)(2,1)S(1)}, u32[]{:S(2)}, u32[]{:S(2)}) collective-permute-start(bf16[1,1,64,320]{3,2,1,0:T(8,128)(2,1)S(1)} %get-tuple-element.30), channel_id=1, source_target_pairs={{0,1},{1,2},{2,3},{3,4},{4,5},{5,6},{6,7},{8,9},{9,10},{10,11},{11... | collective-permute-start | bytes 122888 | tf_op jit(solution)/shard_map/ppermute | solution.py:44
  336.3 5.4 %collective-permute-start.7 = (bf16[1,1,64,320]{3,2,1,0:T(8,128)(2,1)S(1)}, bf16[1,1,64,320]{3,2,1,0:T(8,128)(2,1)S(1)}, u32[]{:S(2)}, u32[]{:S(2)}) collective-permute-start(bf16[1,1,64,320]{3,2,1,0:T(8,128)(2,1)S(1)} %get-tuple-element.31), channel_id=1, source_target_pairs={{1,0},{2,1},{3,2},{4,3},{5,4},{6,5},{7,6},{9,8},{10,9},{11,10},{12... | collective-permute-start | bytes 122888 | tf_op jit(solution)/shard_map/ppermute | solution.py:46
  (1 other events, 5.0 us)
Sparse Core Ops, SparseCore 0:
  11.9 189.5 all-gather.5
  267.6 39.4 all-gather.3
where the time goes:
time: 353 us; the launch traced here: 351 us
  waiting for transfers between devices  170 us (48%)
  starting transfers between devices  55 us (16%)
  matrix products  38.7 us (11%)
  local copies, waits for them, and re-layouts  31.1 us (9%)
  blocking collectives  29.4 us (8%)
  between operations  16.2 us (5%)
  other arithmetic  11.2 us (3%)
    all_gather x1, waiting for transfers between devices, turned_gather(): filled = lax.all_gather(both, axis, axis=0, tiled=True)  89.3 us
    all_gather x1, waiting for transfers between devices, in_one_piece(): filled = lax.all_gather(both, axis, axis=dim, tiled=True)  38.4 us
    all_to_all x3, blocking collectives, from_everyone(): lax.all_to_all(jnp.broadcast_to(shard[None], (length, *shard.shape)), axi...  29.4 us
    all_to_all x3, waiting for transfers between devices, from_everyone(): lax.all_to_all(jnp.broadcast_to(shard[None], (length, *shard.shape)), axi...  25 us
    all_to_all x3, starting transfers between devices, from_everyone(): lax.all_to_all(jnp.broadcast_to(shard[None], (length, *shard.shape)), axi...  24 us
    dot_general x36, matrix products, convolve(): jnp.einsum('bhwc,cd->bhwd', window, kernel[offset * width_in:(offset + 1)...  22.1 us
    unnamed x28, local copies, waits for them, and re-layouts  16.4 us
    ppermute x4, starting transfers between devices, extended(): lax.ppermute(tail, axis, [(i, (i + 1) % count) for i in range(ends)])  12.9 us
  transfers between devices with their start and end apart: 14, of which 8 were waited for; matrix products, arithmetic and copies ran while one was open for 6% of the time, Pallas kernels for 0%

commit v1 on v0

--- a/solution.py
+++ b/solution.py
@@ -4,6 +4,8 @@
 import jax.numpy as jnp
 from jax import lax
 from jax.sharding import PartitionSpec as P
+from jax.experimental import pallas as pl
+from jax.experimental.pallas import tpu as pltpu
 
 HEADS = 8
 HEAD_SIZE = 40
@@ -116,6 +118,139 @@
     bias_two = lax.dynamic_slice_in_dim(second_bias, position * width_two, width_two, 0)
     columns = jnp.dot(hidden_all, second, preferred_element_type=jnp.float32) + bias_two
     return lax.all_to_all(columns, "batch", split_axis=0, concat_axis=1, tiled=True)
+
+
+CHUNKS = 8
+CHUNK = 1408
+OWN = CHUNKS // 2
+MESH = pl.DeviceIdType.MESH
+
+
+def widened(turned, width):
+    return jnp.pad(turned, ((0, 0), (0, width - turned.shape[1])))
+
+
+def piece_of(first, second, convs, squares):
+    tf = first.T.reshape(4, 5, 320).transpose(1, 0, 2)
+    tf = jnp.pad(tf, ((0, 0), (0, 0), (0, 64))).reshape(5, 1536)
+    ts = second.T.reshape(5, 64, 4, 5).transpose(0, 2, 1, 3).reshape(5, 4, 320)
+    ts = jnp.pad(ts, ((0, 0), (0, 0), (0, 64))).reshape(5, 1536)
+    rows = [tf, ts] + [widened(c.T, 2944) for c in convs] + [widened(m.T, 384) for m in squares]
+    rows = jnp.concatenate(rows, axis=1)
+    rows = jnp.pad(rows, ((0, 3), (0, 0)))
+    return rows.reshape(8, CHUNKS, CHUNK).transpose(1, 0, 2)
+
+
+def gather_kernel(piece, w, y_s, y_r, z_s, z_r, x_s, x_r, c_s, c_r):
+    b = lax.axis_index("batch")
+    s = lax.axis_index("space")
+    yh = lax.rem(b, 2)
+    z = lax.rem(lax.div(b, 2), 8)
+    x = lax.div(b, 16)
+    core = lax.rem(s, 2)
+    sib = s + 1 - 2 * core
+    mate = b + 1 - 2 * yh
+
+    def at_z(zz):
+        return (x * 8 + zz) * 2 + yh
+
+    def at_x(xx):
+        return (xx * 8 + z) * 2 + yh
+
+    zs = [lax.rem(z + d, 8) for d in range(8)]
+    xs = [lax.rem(x + d, 4) for d in range(4)]
+    z_from = [lax.rem(z + 8 - d, 8) for d in range(8)]
+    x_from = [lax.rem(x + 4 - d, 4) for d in range(4)]
+
+    barrier = pltpu.get_barrier_semaphore()
+    for dev in [(mate, s), (b, sib)] + [(at_z(q), s) for q in zs[1:]] + [(at_x(q), s) for q in xs[1:]]:
+        pl.semaphore_signal(barrier, inc=1, device_id=dev, device_id_type=MESH)
+    for i in range(OWN):
+        w[2 * i + core, b] = piece[2 * i + core]
+    pl.semaphore_wait(barrier, 12)
+
+    def send(src, dst, ss, rs, dev):
+        return pltpu.make_async_remote_copy(
+            src_ref=src, dst_ref=dst, send_sem=ss, recv_sem=rs, device_id=dev, device_id_type=MESH
+        )
+
+    ys, zc, xc, cc = [], {}, {}, {}
+    for i in range(OWN):
+        c = 2 * i + core
+        copy = send(piece.at[c], w.at[c, b], y_s.at[i], y_r.at[i], (mate, s))
+        copy.start()
+        ys.append(copy)
+    pair = b - yh
+    for i in range(OWN):
+        c = 2 * i + core
+        ys[i].wait_recv()
+        for d in range(1, 8):
+            part = w.at[c, pl.ds(pair, 2)]
+            copy = send(part, part, z_s.at[i, d - 1], z_r.at[i, d - 1], (at_z(zs[d]), s))
+            copy.start()
+            zc[i, d] = copy
+    for i in range(OWN):
+        c = 2 * i + core
+        for d in range(1, 8):
+            zc[i, d].wait_recv()
+        block = w.at[c, pl.ds(x * 16, 16)]
+        for d in range(1, 4):
+            copy = send(block, block, x_s.at[i, d - 1], x_r.at[i, d - 1], (at_x(xs[d]), s))
+            copy.start()
+            xc[i, d] = copy
+        copy = send(block, block, c_s.at[i, 0], c_r.at[i, 0], (b, sib))
+        copy.start()
+        cc[i, 0] = copy
+    for i in range(OWN):
+        c = 2 * i + core
+        for d in range(1, 4):
+            xc[i, d].wait_recv()
+            block = w.at[c, pl.ds(x_from[d] * 16, 16)]
+            copy = send(block, block, c_s.at[i, d], c_r.at[i, d], (b, sib))
+            copy.start()
+            cc[i, d] = copy
+    for i in range(OWN):
+        for d in range(4):
+            cc[i, d].wait_recv()
+    for i in range(OWN):
+        ys[i].wait_send()
+        for d in range(1, 8):
+            zc[i, d].wait_send()
+        for d in range(1, 4):
+            xc[i, d].wait_send()
+        for d in range(4):
+            cc[i, d].wait_send()
+
+
+def gather_weights(piece):
+    dma = pltpu.SemaphoreType.DMA
+    return pl.pallas_call(
+        gather_kernel,
+        out_shape=jax.ShapeDtypeStruct((CHUNKS, 64, 8, CHUNK), jnp.bfloat16),
+        in_specs=[pl.BlockSpec(memory_space=pltpu.VMEM)],
+        out_specs=pl.BlockSpec(memory_space=pltpu.VMEM),
+        scratch_shapes=[
+            dma((OWN,)),
+            dma((OWN,)),
+            dma((OWN, 7)),
+            dma((OWN, 7)),
+            dma((OWN, 3)),
+            dma((OWN, 3)),
+            dma((OWN, 4)),
+            dma((OWN, 4)),
+        ],
+        compiler_params=pltpu.CompilerParams(collective_id=0, has_side_effects=True, vmem_limit_bytes=40 << 20),
+        name="gather_weights",
+    )(piece)
+
+
+def embed_local(timesteps, tf, first_bias, ts, second_bias):
+    wave = waveform_of(timesteps, 160)
+    inner = jnp.einsum("vk,bjik->vbij", wave, tf, preferred_element_type=jnp.float32)
+    inner = jax.nn.silu(inner.reshape(1, 1280) + first_bias)
+    hidden = jax.nn.silu(inner).astype(jnp.bfloat16)
+    hidden = hidden.reshape(1, 64, 4, 5).transpose(0, 2, 1, 3).reshape(1, 4, 320)
+    return jnp.einsum("vik,nik->vn", hidden, ts, preferred_element_type=jnp.float32) + second_bias
 
 
 def convolve(padded, kernel):
@@ -231,22 +366,23 @@
     final_gain,
     layer_gain,
 ):
-    gathered = turned_gather(
-        (
-            conv_first,
-            conv_second,
-            proj_inner,
-            query_weight,
-            key_weight,
-            value_weight,
-            attn_out,
-            proj_outer,
-        ),
-        "batch",
-        (1, 1, 1, 1, 1, 1, 1, 1),
-    )
-    conv_one, conv_two, inner_w, query_w, key_w, value_w, output_w, outer_w = gathered
-    embedded = embed_sharded(timesteps, time_first, time_first_bias, time_second, time_second_bias)
+    piece = piece_of(
+        time_first,
+        time_second,
+        (conv_first, conv_second),
+        (proj_inner, query_weight, key_weight, value_weight, attn_out, proj_outer),
+    )
+    whole = gather_weights(piece)
+    whole = whole.transpose(1, 2, 0, 3).reshape(64, 8, CHUNKS * CHUNK)[:, :5]
+    tf = whole[:, :, :1536].reshape(64, 5, 4, 384)[..., :320]
+    whole = whole.reshape(320, CHUNKS * CHUNK)
+    ts = whole[:, 1536:3072].reshape(320, 4, 384)[..., :320]
+    conv_one = whole[:, 3072 : 3072 + 2880].T
+    conv_two = whole[:, 6016 : 6016 + 2880].T
+    inner_w, query_w, key_w, value_w, output_w, outer_w = (
+        whole[:, 8960 + 384 * i : 8960 + 384 * i + 320].T for i in range(6)
+    )
+    embedded = embed_local(timesteps, tf, time_first_bias, ts, time_second_bias)
     alpha_bar = lookup(timesteps)[:, None, None, None]
     noisy = (jnp.sqrt(alpha_bar) * latents + jnp.sqrt(1.0 - alpha_bar) * noise_draw).astype(
         jnp.bfloat16

time: 353 us -> 297 us (0.84)
  waiting for transfers between devices: 170 us -> 45.3 us
  Pallas kernels: 0 us -> 91.7 us
  starting transfers between devices: 55 us -> 27.7 us
  local copies, waits for them, and re-layouts: 31.1 us -> 45.8 us
  blocking collectives: 29.4 us -> 23.8 us
  matrix products: 38.7 us -> 34.4 us
    pallas_call x0 -> x1, Pallas kernels: none -> 91.7 us  [gather_weights(): pl.pallas_call(gather_kernel, out_shape=jax.ShapeDtypeStruct((CHUNKS, 64,...]
    all_gather x1 -> x0, waiting for transfers between devices: 89.3 us -> none  [turned_gather(): filled = lax.all_gather(both, axis, axis=0, tiled=True)]
    all_to_all x3 -> x1, waiting for transfers between devices: 25 us -> 3.19 us  [from_everyone(): lax.all_to_all(jnp.broadcast_to(shard[None], (length, *shard.shape)), axi...]
    all_to_all x3 -> x1, starting transfers between devices: 24 us -> 3.29 us  [from_everyone(): lax.all_to_all(jnp.broadcast_to(shard[None], (length, *shard.shape)), axi...]
    reshape x2 -> x10, local copies, waits for them, and re-layouts: 0.13 us -> 19.5 us  [the longest x1 10.6 us: body(): whole = whole.reshape(320, CHUNKS * CHUNK)]
    all_to_all x1 -> x0, waiting for transfers between devices: 12.9 us -> none  [embed_sharded(): lax.all_to_all(columns, 'batch', split_axis=0, concat_axis=1, tiled=True)]
    all_to_all x1 -> x0, starting transfers between devices: 6.65 us -> none  [embed_sharded(): lax.all_to_all(columns, 'batch', split_axis=0, concat_axis=1, tiled=True)]
    all_to_all x3, blocking collectives: 29.4 us -> 23.8 us  [from_everyone(): lax.all_to_all(jnp.broadcast_to(shard[None], (length, *shard.shape)), axi...]
  transfers between devices with their start and end apart: 14 -> 10, of which waited for: 8 -> 4; matrix products, arithmetic and copies ran while one was open for 6% -> 13% of each run, Pallas kernels for 0% -> 31%
where the time goes in v1:
time: 297 us; the launch traced here: 295 us
  Pallas kernels  91.7 us (31%)
  local copies, waits for them, and re-layouts  45.8 us (15%)
  waiting for transfers between devices  45.3 us (15%)
  matrix products  34.4 us (12%)
  starting transfers between devices  27.7 us (9%)
  blocking collectives  23.8 us (8%)
  between operations  16.4 us (6%)
  other arithmetic  10.4 us (4%)
    pallas_call x1, Pallas kernels, gather_weights(): pl.pallas_call(gather_kernel, out_shape=jax.ShapeDtypeStruct((CHUNKS, 64,...  91.7 us
    all_gather x1, waiting for transfers between devices, in_one_piece(): filled = lax.all_gather(both, axis, axis=dim, tiled=True)  37.9 us
    all_to_all x3, blocking collectives, from_everyone(): lax.all_to_all(jnp.broadcast_to(shard[None], (length, *shard.shape)), axi...  23.8 us
    dot_general x36, matrix products, convolve(): jnp.einsum('bhwc,cd->bhwd', window, kernel[offset * width_in:(offset + 1)...  17.9 us
    unnamed x45, local copies, waits for them, and re-layouts  16.2 us
    ppermute x4, starting transfers between devices, extended(): lax.ppermute(tail, axis, [(i, (i + 1) % count) for i in range(ends)])  12.9 us
    ppermute x4, starting transfers between devices, extended(): lax.ppermute(head, axis, [((i + 1) % count, i) for i in range(ends)])  11.4 us
    reshape x1, local copies, waits for them, and re-layouts, body(): whole = whole.reshape(320, CHUNKS * CHUNK)  10.6 us
  transfers between devices with their start and end apart: 10, of which 4 were waited for; matrix products, arithmetic and copies ran while one was open for 13% of the time, Pallas kernels for 31%

profile of v1, /device:TPU:1, one launch (start us, length us, event | category | flops | bytes accessed | tf_op | source)
XLA Modules:
  0.0 295.5 jit_solution(4028991685860828324)
XLA Ops:
  10.7 4.6 %collective-permute-start = (bf16[1,1,64,4]{2,3,1,0:T(4,128)(2,1)S(1)}, bf16[1,1,64,4]{2,3,1,0:T(4,128)(2,1)S(1)}, u32[]{:S(2)}, u32[]{:S(2)}) collective-permute-start(bf16[1,1,64,4]{2,3,1,0:T(4,128)(2,1)S(1)} %get-tuple-element.37), channel_id=1, source_target_pairs={{0,1},{1,2},{2,3},{3,4},{4,5},{5,6},{6,7},{8,9},{9,10},{10,11},{11... | collective-permute-start | bytes 1544 | tf_op jit(solution)/shard_map/ppermute | solution.py:46
  15.3 5.5 %collective-permute-start.1 = (bf16[1,1,64,4]{2,3,1,0:T(4,128)(2,1)S(1)}, bf16[1,1,64,4]{2,3,1,0:T(4,128)(2,1)S(1)}, u32[]{:S(2)}, u32[]{:S(2)}) collective-permute-start(bf16[1,1,64,4]{2,3,1,0:T(4,128)(2,1)S(1)} %get-tuple-element.38), channel_id=1, source_target_pairs={{1,0},{2,1},{3,2},{4,3},{5,4},{6,5},{7,6},{9,8},{10,9},{11,10},{12... | collective-permute-start | bytes 1544 | tf_op jit(solution)/shard_map/ppermute | solution.py:48
  29.3 91.7 %gather_weights.1 = bf16[8,64,8,1408]{3,2,1,0:T(8,128)(2,1)S(1)} custom-call(bf16[8,8,1408]{2,1,0:T(8,128)(2,1)S(1)} %bitcast.336), custom_call_target="tpu_custom_call" | custom-call | tf_op jit(solution)/shard_map/gather_weights/pallas_call | solution.py:227
  121.1 3.5 %copy.68 = bf16[8,64,1,8,1408]{4,3,0,2,1:T(8,128)(2,1)S(1)} copy(bf16[8,64,1,8,1408]{4,3,2,1,0:T(8,128)(2,1)S(1)} %bitcast.335) | data formatting | bytes 23068672 | tf_op jit(solution)/shard_map/reshape | solution.py:376
  124.5 4.3 %copy-done = bf16[8,64,1,8,1408]{4,3,0,2,1:T(8,128)(2,1)} copy-done((bf16[8,64,1,8,1408]{4,3,0,2,1:T(8,128)(2,1)}, bf16[8,64,1,8,1408]{4,3,0,2,1:T(8,128)(2,1)S(1)}, u32[]{:S(2)}) %copy-start) | copy-done | bytes 11534360
  130.4 10.6 %reshape.886 = bf16[320,11264]{1,0:T(8,128)(2,1)} reshape(bf16[64,5,11264]{2,1,0:T(8,128)(2,1)} %bitcast.338) | data formatting | bytes 14417920 | tf_op jit(solution)/shard_map/reshape | solution.py:378
  141.0 3.7 %fusion.182 = (bf16[320,2880]{1,0:T(8,128)(2,1)}, bf16[320,2880]{1,0:T(8,128)(2,1)S(1)}) fusion(bf16[320,11264]{1,0:T(8,128)(2,1)} %reshape.886), kind=kLoop, calls=%fused_computation.306 | loop fusion | bytes 7372800 | tf_op jit(solution)/shard_map/slice | solution.py:380
  149.5 3.3 %all-to-all-start = ((f32[8,1,64]{2,1,0:T(1,128)}), f32[8,1,64]{2,1,0:T(1,128)S(1)}, u32[]{:S(2)}, u32[]{:S(2)}) async-start(f32[8,1,64]{2,1,0:T(1,128)} %broadcast_in_dim.17), calls=%async_computation | async-start | bytes 8192 | tf_op jit(solution)/shard_map/all_to_all | solution.py:29
  154.5 3.2 %all-to-all-done = f32[8,1,64]{2,1,0:T(1,128)S(1)} async-done(((f32[8,1,64]{2,1,0:T(1,128)}), f32[8,1,64]{2,1,0:T(1,128)S(1)}, u32[]{:S(2)}, u32[]{:S(2)}) %all-to-all-start) | async-done | bytes 2080 | tf_op jit(solution)/shard_map/all_to_all | solution.py:29
  158.3 2.8 collective-permute-start.2
  161.1 1.9 collective-permute-start.3
  163.0 1.6 convolution_reduce_fusion
  164.6 4.0 %copy.64 = bf16[320,2880]{0,1:T(8,128)(2,1)} copy(bf16[320,2880]{1,0:T(8,128)(2,1)} %get-tuple-element.20) | data formatting | bytes 3686400
  175.8 8.1 %all_to_all.24 = f32[8,1,64]{2,1,0:T(1,128)S(1)} all-to-all(f32[8,1,64]{2,1,0:T(1,128)S(1)} %broadcast_in_dim.18), channel_id=1, replica_groups=mesh['batch'=64,'space'=8] {'space'}, dimensions={0} | all-to-all | bytes 4096 | tf_op jit(solution)/shard_map/all_to_all | solution.py:29
  184.5 2.8 collective-permute-start.4
  187.3 2.1 collective-permute-start.5
  189.4 2.6 copy.66
  199.7 7.6 %all_to_all.25 = f32[8,1,64]{2,1,0:T(1,128)S(1)} all-to-all(f32[8,1,64]{2,1,0:T(1,128)S(1)} %broadcast_in_dim.20), channel_id=1, replica_groups=mesh['batch'=64,'space'=8] {'space'}, dimensions={0} | all-to-all | bytes 4096 | tf_op jit(solution)/shard_map/all_to_all | solution.py:29
  213.5 37.9 %all-gather.2.cloned.1.call-done = bf16[2,2048,320]{1,2,0:T(8,128)(2,1)} async-done(((bf16[2,256,320]{1,2,0:T(8,128)(2,1)}), bf16[2,2048,320]{1,2,0:T(8,128)(2,1)}) %all-gather.2.cloned.1.call-update) | async-done | bytes 2621456 | tf_op jit(solution)/shard_map/all_gather | solution.py:72
  251.4 1.9 fusion.183
  268.8 8.2 %all_to_all.26 = f32[8,1,64]{2,1,0:T(1,128)S(1)} all-to-all(f32[8,1,64]{2,1,0:T(1,128)S(1)} %broadcast_in_dim.22), channel_id=1, replica_groups=mesh['batch'=64,'space'=8] {'space'}, dimensions={0} | all-to-all | bytes 4096 | tf_op jit(solution)/shard_map/all_to_all | solution.py:29
  277.6 2.8 collective-permute-start.6
  280.4 1.9 collective-permute-start.7
  282.4 3.5 %collective-permute-done.7 = bf16[1,1,64,320]{3,2,1,0:T(8,128)(2,1)S(1)} collective-permute-done((bf16[1,1,64,320]{3,2,1,0:T(8,128)(2,1)S(1)}, bf16[1,1,64,320]{3,2,1,0:T(8,128)(2,1)S(1)}, u32[]{:S(2)}, u32[]{:S(2)}) %collective-permute-start.7) | collective-permute-done | bytes 40992 | tf_op jit(solution)/shard_map/ppermute | solution.py:48
  (206 shorter events, 59.2 us)
Async XLA Ops:
  10.7 135.0 %collective-permute-start = (bf16[1,1,64,4]{2,3,1,0:T(4,128)(2,1)S(1)}, bf16[1,1,64,4]{2,3,1,0:T(4,128)(2,1)S(1)}, u32[]{:S(2)}, u32[]{:S(2)}) collective-permute-start(bf16[1,1,64,4]{2,3,1,0:T(4,128)(2,1)S(1)} %get-tuple-element.37), channel_id=1, source_target_pairs={{0,1},{1,2},{2,3},{3,4},{4,5},{5,6},{6,7},{8,9},{9,10},{10,11},{11... | collective-permute-start | bytes 1544 | tf_op jit(solution)/shard_map/ppermute | solution.py:46
  15.3 130.4 %collective-permute-start.1 = (bf16[1,1,64,4]{2,3,1,0:T(4,128)(2,1)S(1)}, bf16[1,1,64,4]{2,3,1,0:T(4,128)(2,1)S(1)}, u32[]{:S(2)}, u32[]{:S(2)}) collective-permute-start(bf16[1,1,64,4]{2,3,1,0:T(4,128)(2,1)S(1)} %get-tuple-element.38), channel_id=1, source_target_pairs={{1,0},{2,1},{3,2},{4,3},{5,4},{6,5},{7,6},{9,8},{10,9},{11,10},{12... | collective-permute-start | bytes 1544 | tf_op jit(solution)/shard_map/ppermute | solution.py:48
  124.5 4.4 %copy-start = (bf16[8,64,1,8,1408]{4,3,0,2,1:T(8,128)(2,1)}, bf16[8,64,1,8,1408]{4,3,0,2,1:T(8,128)(2,1)S(1)}, u32[]{:S(2)}) copy-start(bf16[8,64,1,8,1408]{4,3,0,2,1:T(8,128)(2,1)S(1)} %copy.68) | copy-start | bytes 34603012
  141.0 4.8 %copy-start.4 = (bf16[36,320]{1,0:T(8,128)(2,1)S(1)}, bf16[36,320]{1,0:T(8,128)(2,1)}, u32[]{:S(2)}) copy-start(bf16[36,320]{1,0:T(8,128)(2,1)} %param.25) | copy-start | bytes 69124
  144.7 8.2 %copy-start.5 = (f32[1280]{0:T(1024)S(1)}, f32[1280]{0:T(1024)}, u32[]{:S(2)}) copy-start(f32[1280]{0:T(1024)} %param.27) | copy-start | bytes 15364
  146.3 7.0 %slice-start.2 = ((bf16[320,11264]{1,0:T(8,128)(2,1)}), bf16[320,1536]{1,0:T(8,128)(2,1)S(1)}, s32[]{:S(2)}) async-start(bf16[320,11264]{1,0:T(8,128)(2,1)} %reshape.886), calls=%async_computation.7 | async-start | bytes 1966080 | tf_op jit(solution)/shard_map/slice | solution.py:379
  147.0 11.2 %copy-start.7 = (f32[320]{0:T(512)S(1)}, f32[320]{0:T(512)}, u32[]{:S(2)}) copy-start(f32[320]{0:T(512)} %param.39) | copy-start | bytes 3844
  149.5 8.1 %all-to-all-start = ((f32[8,1,64]{2,1,0:T(1,128)}), f32[8,1,64]{2,1,0:T(1,128)S(1)}, u32[]{:S(2)}, u32[]{:S(2)}) async-start(f32[8,1,64]{2,1,0:T(1,128)} %broadcast_in_dim.17), calls=%async_computation | async-start | bytes 8192 | tf_op jit(solution)/shard_map/all_to_all | solution.py:29
  152.8 98.6 %all-gather.2.cloned.1.call-start = ((), (), s32[]{:S(2)}) async-start(), calls=%async_computation.4 | async-start | bytes 2949120 | tf_op jit(solution)/shard_map/all_gather | solution.py:72
  152.9 15.7 %copy-start.12 = (f32[320]{0:T(512)S(1)}, f32[320]{0:T(512)}, u32[]{:S(2)}) copy-start(f32[320]{0:T(512)} %param.29) | copy-start | bytes 3844
  158.3 10.3 %collective-permute-start.2 = (bf16[1,1,64,320]{3,2,1,0:T(8,128)(2,1)S(1)}, bf16[1,1,64,320]{3,2,1,0:T(8,128)(2,1)S(1)}, u32[]{:S(2)}, u32[]{:S(2)}) collective-permute-start(bf16[1,1,64,320]{3,2,1,0:T(8,128)(2,1)S(1)} %get-tuple-element.34), channel_id=1, source_target_pairs={{0,1},{1,2},{2,3},{3,4},{4,5},{5,6},{6,7},{8,9},{9,10},{10,11},{11... | collective-permute-start | bytes 122888 | tf_op jit(solution)/shard_map/ppermute | solution.py:46
  161.1 7.5 %collective-permute-start.3 = (bf16[1,1,64,320]{3,2,1,0:T(8,128)(2,1)S(1)}, bf16[1,1,64,320]{3,2,1,0:T(8,128)(2,1)S(1)}, u32[]{:S(2)}, u32[]{:S(2)}) collective-permute-start(bf16[1,1,64,320]{3,2,1,0:T(8,128)(2,1)S(1)} %get-tuple-element.35), channel_id=1, source_target_pairs={{1,0},{2,1},{3,2},{4,3},{5,4},{6,5},{7,6},{9,8},{10,9},{11,10},{12... | collective-permute-start | bytes 122888 | tf_op jit(solution)/shard_map/ppermute | solution.py:48
  168.6 5.1 %copy-start.1 = (bf16[320,2880]{0,1:T(8,128)(2,1)S(1)}, bf16[320,2880]{0,1:T(8,128)(2,1)}, u32[]{:S(2)}) copy-start(bf16[320,2880]{0,1:T(8,128)(2,1)} %copy.64) | copy-start | bytes 5529604
  173.8 10.5 %copy-start.8 = (f32[320]{0:T(512)S(1)}, f32[320]{0:T(512)}, u32[]{:S(2)}) copy-start(f32[320]{0:T(512)} %param.40) | copy-start | bytes 3844
  184.5 7.5 %collective-permute-start.4 = (bf16[1,1,64,320]{3,2,1,0:T(8,128)(2,1)S(1)}, bf16[1,1,64,320]{3,2,1,0:T(8,128)(2,1)S(1)}, u32[]{:S(2)}, u32[]{:S(2)}) collective-permute-start(bf16[1,1,64,320]{3,2,1,0:T(8,128)(2,1)S(1)} %get-tuple-element.32), channel_id=1, source_target_pairs={{0,1},{1,2},{2,3},{3,4},{4,5},{5,6},{6,7},{8,9},{9,10},{10,11},{11... | collective-permute-start | bytes 122888 | tf_op jit(solution)/shard_map/ppermute | solution.py:46
  187.3 5.4 %collective-permute-start.5 = (bf16[1,1,64,320]{3,2,1,0:T(8,128)(2,1)S(1)}, bf16[1,1,64,320]{3,2,1,0:T(8,128)(2,1)S(1)}, u32[]{:S(2)}, u32[]{:S(2)}) collective-permute-start(bf16[1,1,64,320]{3,2,1,0:T(8,128)(2,1)S(1)} %get-tuple-element.33), channel_id=1, source_target_pairs={{1,0},{2,1},{3,2},{4,3},{5,4},{6,5},{7,6},{9,8},{10,9},{11,10},{12... | collective-permute-start | bytes 122888 | tf_op jit(solution)/shard_map/ppermute | solution.py:48
  192.0 5.7 %copy-start.2 = (bf16[320,2880]{0,1:T(8,128)(2,1)S(1)}, bf16[320,2880]{0,1:T(8,128)(2,1)}, u32[]{:S(2)}) copy-start(bf16[320,2880]{0,1:T(8,128)(2,1)} %copy.66) | copy-start | bytes 5529604
  197.7 10.0 %copy-start.9 = (f32[320]{0:T(512)S(1)}, f32[320]{0:T(512)}, u32[]{:S(2)}) copy-start(f32[320]{0:T(512)} %param.41) | copy-start | bytes 3844
  198.0 11.1 %copy-start.10 = (f32[320]{0:T(512)S(1)}, f32[320]{0:T(512)}, u32[]{:S(2)}) copy-start(f32[320]{0:T(512)} %param.43) | copy-start | bytes 3844
  265.5 12.0 %copy-start.11 = (f32[320]{0:T(512)S(1)}, f32[320]{0:T(512)}, u32[]{:S(2)}) copy-start(f32[320]{0:T(512)} %param.42) | copy-start | bytes 3844
  265.5 20.4 %copy-start.13 = (bf16[2880,4]{0,1:T(4,128)(2,1)S(1)}, bf16[2880,4]{0,1:T(4,128)(2,1)}, u32[]{:S(2)}) copy-start(bf16[2880,4]{0,1:T(4,128)(2,1)} %param.38) | copy-start | bytes 69124
  266.6 21.2 %copy-start.6 = (f32[1,4,64,4]{2,3,1,0:T(4,128)S(1)}, f32[1,4,64,4]{2,3,1,0:T(4,128)}, u32[]{:S(2)}) copy-start(f32[1,4,64,4]{2,3,1,0:T(4,128)} %param.23) | copy-start | bytes 12292
  277.6 4.7 %collective-permute-start.6 = (bf16[1,1,64,320]{3,2,1,0:T(8,128)(2,1)S(1)}, bf16[1,1,64,320]{3,2,1,0:T(8,128)(2,1)S(1)}, u32[]{:S(2)}, u32[]{:S(2)}) collective-permute-start(bf16[1,1,64,320]{3,2,1,0:T(8,128)(2,1)S(1)} %get-tuple-element.30), channel_id=1, source_target_pairs={{0,1},{1,2},{2,3},{3,4},{4,5},{5,6},{6,7},{8,9},{9,10},{10,11},{11... | collective-permute-start | bytes 122888 | tf_op jit(solution)/shard_map/ppermute | solution.py:46
  280.4 5.4 %collective-permute-start.7 = (bf16[1,1,64,320]{3,2,1,0:T(8,128)(2,1)S(1)}, bf16[1,1,64,320]{3,2,1,0:T(8,128)(2,1)S(1)}, u32[]{:S(2)}, u32[]{:S(2)}) collective-permute-start(bf16[1,1,64,320]{3,2,1,0:T(8,128)(2,1)S(1)} %get-tuple-element.31), channel_id=1, source_target_pairs={{1,0},{2,1},{3,2},{4,3},{5,4},{6,5},{7,6},{9,8},{10,9},{11,10},{12... | collective-permute-start | bytes 122888 | tf_op jit(solution)/shard_map/ppermute | solution.py:48
  (3 other events, 9.6 us)
Sparse Core Ops, SparseCore 0:
  212.5 38.9 all-gather.1

commit v2 on v1

v2 whole, which is shorter than its diff:
```python
import math

import jax
import jax.numpy as jnp
from jax import lax
from jax.experimental import pallas as pl
from jax.experimental.pallas import tpu as pltpu
from jax.sharding import PartitionSpec as P

HEADS = 8
HEAD_SIZE = 40
GROUPS = 32
STEPS = 1000


EPS_GROUP = 1e-06
EPS_BLOCK = 1e-05
EPS_LAYER = 1e-05


def plan():
    fraction = jnp.arange(STEPS, dtype=jnp.float32) / (STEPS - 1)
    beta_root = math.sqrt(0.00085) + fraction * (math.sqrt(0.012) - math.sqrt(0.00085))
    return jnp.cumprod(1.0 - beta_root * beta_root)


def lookup(timesteps):
    plan_tab = plan()
    matches = jnp.arange(STEPS, dtype=jnp.int32)[None, :] == timesteps[:, None]
    return jnp.sum(jnp.where(matches, plan_tab[None, :], 0.0), axis=1)


def waveform_of(timesteps, halfway):
    frequency = jnp.exp(-math.log(10000.0) * jnp.arange(halfway, dtype=jnp.float32) / halfway)
    angles = timesteps.astype(jnp.float32)[:, None] * frequency[None, :]
    return jnp.concatenate([jnp.cos(angles), jnp.sin(angles)], axis=1).astype(jnp.bfloat16)


C = 320
WIDE = 512
ROW = 64
OWN_TOKENS = 256
EDGED = OWN_TOKENS + 2 * ROW
TAPS = 2944
CHUNKS = 8
CHUNK = 1408
OWN = CHUNKS // 2
AT_FIRST = 0
AT_SECOND = 1536
AT_CONV_ONE = 3072
AT_CONV_TWO = 6016
AT_INNER, AT_QUERY, AT_KEY, AT_VALUE, AT_MIX, AT_OUTER = (8960 + 384 * i for i in range(6))
MESH = pl.DeviceIdType.MESH
F32 = jnp.float32
BF16 = jnp.bfloat16


def widened(turned, width):
    return jnp.pad(turned, ((0, 0), (0, width - turned.shape[1])))


def piece_of(first, second, convs, squares):
    tf = first.T.reshape(4, 5, C).transpose(1, 0, 2)
    tf = jnp.pad(tf, ((0, 0), (0, 0), (0, 64))).reshape(5, 1536)
    ts = second.T.reshape(5, 64, 4, 5).transpose(0, 2, 1, 3).reshape(5, 4, C)
    ts = jnp.pad(ts, ((0, 0), (0, 0), (0, 64))).reshape(5, 1536)
    rows = [tf, ts] + [widened(c.T, TAPS) for c in convs] + [widened(m.T, 384) for m in squares]
    rows = jnp.concatenate(rows, axis=1)
    rows = jnp.pad(rows, ((0, 3), (0, 0)))
    return rows.reshape(8, CHUNKS, CHUNK).transpose(1, 0, 2)


def mm(a, b):
    return lax.dot_general(a, b, (((1,), (0,)), ((), ())), preferred_element_type=F32)


def mt(a, b):
    return lax.dot_general(a, b, (((1,), (1,)), ((), ())), preferred_element_type=F32)


def exactly(product, v, matrix):
    high = v.astype(BF16)
    rest = v - high.astype(F32)
    mid = rest.astype(BF16)
    low = (rest - mid.astype(F32)).astype(BF16)
    return product(high, matrix) + product(mid, matrix) + product(low, matrix)


def silu(v):
    half = 0.5 * v
    return half + half * jnp.tanh(half)


def block_kernel(
    piece,
    nt,
    wave,
    vecs,
    win,
    wout,
    out,
    w,
    wn,
    taps,
    xt,
    nview,
    start,
    mid6,
    two6,
    block,
    nat,
    stats,
    spread,
    gwide,
    gslim,
    keys,
    values,
    query,
    base,
    y_s,
    y_r,
    z_s,
    z_r,
    x_s,
    x_r,
    c_s,
    c_r,
    n_s,
    n_r,
    t_s,
    t_r,
    h_s,
    h_r,
    up_s,
    up_r,
    dn_s,
    dn_r,
    k_s,
    k_r,
):
    b = lax.axis_index("batch")
    s = lax.axis_index("space")
    yh = lax.rem(b, 2)
    z = lax.rem(lax.div(b, 2), 8)
    x = lax.div(b, 16)
    core = lax.rem(s, 2)
    chip = lax.div(s, 2)
    sib = s + 1 - 2 * core
    mate = b + 1 - 2 * yh

    def at_z(zz):
        return (x * 8 + zz) * 2 + yh

    def at_x(xx):
        return (xx * 8 + z) * 2 + yh

    zs = [lax.rem(z + d, 8) for d in range(8)]
    xs = [lax.rem(x + d, 4) for d in range(4)]
    x_from = [lax.rem(x + 4 - d, 4) for d in range(4)]
    peers = [lax.rem(s + d, 8) for d in range(8)]
    peers_from = [lax.rem(s + 8 - d, 8) for d in range(8)]

    barrier = pltpu.get_barrier_semaphore()
    friends = [(mate, s)] + [(at_z(q), s) for q in zs[1:]] + [(at_x(q), s) for q in xs[1:]]
    friends += [(b, q) for q in peers[1:]]
    for dev in friends:
        pl.semaphore_signal(barrier, inc=1, device_id=dev, device_id_type=MESH)
    for i in range(OWN):
        w[2 * i + core, b] = piece[2 * i + core]
    nview[s] = nt[...]
    pl.semaphore_wait(barrier, len(friends))

    def send(src, dst, ss, rs, dev):
        return pltpu.make_async_remote_copy(
            src_ref=src, dst_ref=dst, send_sem=ss, recv_sem=rs, device_id=dev, device_id_type=MESH
        )

    pending = []
    ys, zc, xc, cc = [], {}, {}, {}
    for i in range(OWN):
        c = 2 * i + core
        copy = send(piece.at[c], w.at[c, b], y_s.at[i], y_r.at[i], (mate, s))
        copy.start()
        ys.append(copy)
        pending.append(copy)
    ns = []
    for d in range(1, 8):
        copy = send(nt, nview.at[s], n_s.at[d - 1], n_r.at[d - 1], (b, peers[d]))
        copy.start()
        ns.append(copy)
        pending.append(copy)

    wide_i = lax.broadcasted_iota(jnp.int32, (WIDE, C), 0)
    slim_j = lax.broadcasted_iota(jnp.int32, (WIDE, C), 1)
    hit = (lax.shift_right_logical(wide_i, 3) * 5 + lax.bitwise_and(wide_i, 7) == slim_j) & (
        lax.bitwise_and(wide_i, 7) < 5
    )
    spread[...] = jnp.where(hit, 1.0, 0.0).astype(BF16)
    gi = lax.broadcasted_iota(jnp.int32, (WIDE, WIDE), 0)
    gj = lax.broadcasted_iota(jnp.int32, (WIDE, WIDE), 1)
    same = lax.shift_right_logical(gi, 4) == lax.shift_right_logical(gj, 4)
    gwide[...] = jnp.where(same, 1.0, 0.0).astype(BF16)
    ni = lax.broadcasted_iota(jnp.int32, (C, C), 0)
    nj = lax.broadcasted_iota(jnp.int32, (C, C), 1)
    apart = ni - lax.div(nj, 10) * 10
    gslim[...] = jnp.where((apart >= 0) & (apart < 10), 1.0, 0.0).astype(BF16)
    wide_vecs = exactly(mt, vecs[...], spread[...])
    win_wide = mt(win[...], spread[...]).astype(BF16)

    for copy in ns:
        copy.wait_recv()
    field = jnp.concatenate([nview[q] for q in range(8)], axis=1).astype(F32)
    token = lax.broadcasted_iota(jnp.int32, (16, 2048), 1)
    above = jnp.where(token < ROW, 0.0, pltpu.roll(field, ROW, 1))
    below = jnp.where(token >= 2048 - ROW, 0.0, pltpu.roll(field, 2048 - ROW, 1))
    rows = jnp.concatenate([above, field, below, jnp.zeros((80, 2048), F32)], axis=0)
    xt[0:ROW, :] = jnp.zeros((ROW, 128), BF16)
    xt[ROW + 2048 : 2 * ROW + 2048, :] = jnp.zeros((ROW, 128), BF16)
    xt[ROW : ROW + 2048, :] = rows.T.astype(BF16)

    pair = b - yh
    for i in range(OWN):
        c = 2 * i + core
        ys[i].wait_recv()
        for d in range(1, 8):
            part = w.at[c, pl.ds(pair, 2)]
            copy = send(part, part, z_s.at[i, d - 1], z_r.at[i, d - 1], (at_z(zs[d]), s))
            copy.start()
            zc[i, d] = copy
            pending.append(copy)

    def start_sums(q, carry):
        total, squared = carry
        part = mm(xt[pl.ds(pl.multiple_of(ROW + q * 256, 64), 256), :], win_wide)
        part = part.astype(BF16).astype(F32)
        return total + jnp.sum(part, axis=0, keepdims=True), squared + jnp.sum(part * part, axis=0, keepdims=True)

    zero = jnp.zeros((1, WIDE), F32)
    total, squared = lax.fori_loop(0, 8, start_sums, (zero, zero))
    start[...] = mm(xt[pl.ds(pl.multiple_of(s * 256, 256), EDGED), :], win_wide).astype(BF16)

    def stacked(total, squared):
        width = total.shape[1]
        return jnp.concatenate([total, squared, jnp.zeros((6, width), F32)], axis=0)

    def affine(sums, groups, gain, epsilon):
        sums = exactly(mm, sums, groups) * (1.0 / 20480.0)
        mean = sums[0:1]
        factor = lax.rsqrt(sums[1:2] - mean * mean + epsilon) * gain
        return factor, -mean * factor

    line = lax.broadcasted_iota(jnp.int32, (EDGED, 1), 0)
    outside = ((s == 0) & (line < ROW)) | ((s == 7) & (line >= EDGED - ROW))
    column = lax.bitwise_and(line, ROW - 1)

    def into_taps(field, factor, shift):
        active = jnp.where(outside, 0.0, silu(field.astype(F32) * factor + shift)).astype(BF16)
        slim = mm(active, spread[...])
        west = jnp.where(column == 0, 0.0, pltpu.roll(slim, 1, 0)).astype(BF16)
        east = jnp.where(column == ROW - 1, 0.0, pltpu.roll(slim, EDGED - 1, 0)).astype(BF16)
        for dx, shifted in enumerate((west, slim.astype(BF16), east)):
            for dy in range(3):
                tap = 3 * dy + dx
                taps[:, tap * C : (tap + 1) * C] = shifted[dy * ROW : dy * ROW + OWN_TOKENS]

    for i in range(OWN):
        c = 2 * i + core
        for d in range(1, 8):
            zc[i, d].wait_recv()
        part = w.at[c, pl.ds(x * 16, 16)]
        for d in range(1, 4):
            copy = send(part, part, x_s.at[i, d - 1], x_r.at[i, d - 1], (at_x(xs[d]), s))
            copy.start()
            xc[i, d] = copy
            pending.append(copy)
        copy = send(part, part, c_s.at[i, 0], c_r.at[i, 0], (b, sib))
        copy.start()
        cc[i, 0] = copy
        pending.append(copy)

    taps[:, 9 * C :] = jnp.zeros((OWN_TOKENS, TAPS - 9 * C), BF16)
    factor, shift = affine(stacked(total, squared), gwide[...], wide_vecs[5:6], EPS_BLOCK)
    into_taps(start[...], factor, shift)

    def arrive(i):
        c = 2 * i + core
        for d in range(1, 4):
            xc[i, d].wait_recv()
            part = w.at[c, pl.ds(x_from[d] * 16, 16)]
            copy = send(part, part, c_s.at[i, d], c_r.at[i, d], (b, sib))
            copy.start()
            cc[i, d] = copy
            pending.append(copy)

    def unpack(i):
        for d in range(4):
            cc[i, d].wait_recv()

        def two(p, _):
            for c in (2 * i, 2 * i + 1):
                both = w[c, pl.ds(2 * p, 2)].astype(F32).reshape(16, CHUNK)
                wn[pl.ds(pl.multiple_of(p * 16, 16), 16), c * CHUNK : (c + 1) * CHUNK] = both.astype(BF16)
            return 0

        lax.fori_loop(0, 32, two, 0)

    arrive(0)
    arrive(1)
    unpack(0)
    unpack(1)
    embedded = wide_vecs[4:5]
    for i in range(4):
        inner = mt(wave[...], wn[:, AT_FIRST + 384 * i : AT_FIRST + 384 * i + C])
        hidden = silu(silu(inner + wide_vecs[i : i + 1])).astype(BF16)
        hidden = mm(hidden, spread[...]).astype(BF16)
        embedded = embedded + mt(hidden, wn[:, AT_SECOND + 384 * i : AT_SECOND + 384 * i + C])[0:1]
    arrive(2)
    unpack(2)
    middle = (mt(taps[...], wn[:, AT_CONV_ONE : AT_CONV_ONE + TAPS]) + embedded).astype(BF16)

    def exchange(layer, field, edged):
        edged[ROW : ROW + OWN_TOKENS, :] = field
        wide = field.astype(F32)
        stats[layer, s] = stacked(jnp.sum(wide, axis=0, keepdims=True), jnp.sum(wide * wide, axis=0, keepdims=True))
        up = send(
            edged.at[pl.ds(ROW, ROW)],
            edged.at[pl.ds(ROW + OWN_TOKENS, ROW)],
            h_s.at[layer, 0],
            h_r.at[layer, 0],
            (b, lax.rem(s + 7, 8)),
        )
        down = send(
            edged.at[pl.ds(OWN_TOKENS, ROW)],
            edged.at[pl.ds(0, ROW)],
            h_s.at[layer, 1],
            h_r.at[layer, 1],
            (b, lax.rem(s + 1, 8)),
        )

        @pl.when(s > 0)
        def _():
            up.start()

        @pl.when(s < 7)
        def _():
            down.start()

        copies = []
        for d in range(1, 8):
            copy = send(
                stats.at[layer, s], stats.at[layer, s], t_s.at[layer, d - 1], t_r.at[layer, d - 1], (b, peers[d])
            )
            copy.start()
            copies.append(copy)
            pending.append(copy)
        return up, down, copies

    def gather_stats(layer, copies):
        for copy in copies:
            copy.wait_recv()
        sums = stats[layer, 0]
        for q in range(1, 8):
            sums = sums + stats[layer, q]
        return sums

    def exchanged(layer, up, down, copies):
        @pl.when(s < 7)
        def _():
            up.wait_recv()

        @pl.when(s > 0)
        def _():
            down.wait_recv()

        @pl.when(s > 0)
        def _():
            up.wait_send()

        @pl.when(s < 7)
        def _():
            down.wait_send()

        return gather_stats(layer, copies)

    swap = exchange(0, middle, mid6)
    arrive(3)
    unpack(3)
    sums = exchanged(0, *swap)
    factor, shift = affine(sums, gwide[...], wide_vecs[6:7], EPS_BLOCK)
    into_taps(mid6[...], factor, shift)
    one = mt(taps[...], wn[:, AT_CONV_TWO : AT_CONV_TWO + TAPS])
    one = (one + start[ROW : ROW + OWN_TOKENS, :].astype(F32)).astype(BF16)
    block[...] = one

    slim = mm(one, spread[...])
    nat[s] = slim.astype(BF16)
    slim_sums = stacked(jnp.sum(slim, axis=0, keepdims=True), jnp.sum(slim * slim, axis=0, keepdims=True))
    stats[2, s] = jnp.concatenate([slim_sums, jnp.zeros((8, WIDE - C), F32)], axis=1)
    copies = []
    for d in range(1, 8):
        copy = send(stats.at[2, s], stats.at[2, s], t_s.at[2, d - 1], t_r.at[2, d - 1], (b, peers[d]))
        copy.start()
        copies.append(copy)
        pending.append(copy)

    def hop(source, towards, ss, rs):
        return send(nat.at[source], nat.at[source], ss, rs, (b, towards))

    def to_sib(source_chip):
        source = 2 * source_chip + core
        return hop(source, sib, k_s.at[source_chip], k_r.at[source_chip])

    first_up = hop(s, lax.rem(s + 2, 8), up_s.at[0], up_r.at[0])
    first_dn = hop(s, lax.rem(s + 6, 8), dn_s.at[0], dn_r.at[0])

    @pl.when(chip < 3)
    def _():
        first_up.start()

    @pl.when(chip > 0)
    def _():
        first_dn.start()

    to_sib(chip).start()

    def ups(h):
        source = s - 2 * h
        here = hop(source, lax.rem(s + 2, 8), up_s.at[min(h, 2)], up_r.at[h - 1])
        on = hop(source, lax.rem(s + 2, 8), up_s.at[min(h, 2)], up_r.at[min(h, 2)])
        return here, on

    def dns(h):
        source = s + 2 * h
        here = hop(source, lax.rem(s + 6, 8), dn_s.at[min(h, 2)], dn_r.at[h - 1])
        on = hop(source, lax.rem(s + 6, 8), dn_s.at[min(h, 2)], dn_r.at[min(h, 2)])
        return here, on

    for h in range(1, 4):

        @pl.when(chip >= h)
        def _(h=h):
            here, on = ups(h)
            here.wait_recv()
            if h < 3:

                @pl.when(chip < 3)
                def _():
                    on.start()

            to_sib(chip - h).start()

        @pl.when(chip + h <= 3)
        def _(h=h):
            here, on = dns(h)
            here.wait_recv()
            if h < 3:

                @pl.when(chip > 0)
                def _():
                    on.start()

            to_sib(chip + h).start()

    for q in range(4):
        source = 2 * q + 1 - core
        hop(source, sib, k_s.at[q], k_r.at[q]).wait_recv()
    sums = gather_stats(2, copies)
    factor, shift = affine(sums[:, :C], gslim[...], vecs[9:10, :], EPS_GROUP)
    lane = lax.broadcasted_iota(jnp.int32, (1, WIDE), 1)
    real = lax.bitwise_and(lane, 7) < 5

    def tokens(q):
        normed = (nat[q].astype(F32) * factor + shift).astype(BF16)
        projected = mt(normed, wn[:, AT_INNER : AT_INNER + C])
        mean = jnp.sum(projected, axis=1, keepdims=True) * (1.0 / C)
        centred = jnp.where(real, projected - mean, 0.0)
        spreadness = jnp.sum(centred * centred, axis=1, keepdims=True) * (1.0 / C)
        inside = (centred * lax.rsqrt(spreadness + EPS_LAYER) * wide_vecs[8:9]).astype(BF16)
        inside = mm(inside, spread[...]).astype(BF16)
        where = pl.ds(pl.multiple_of(q * 256, 256), 256)
        keys[where, :] = mt(inside, wn[:, AT_KEY : AT_KEY + C]).astype(BF16)
        values[where, :] = mt(inside, wn[:, AT_VALUE : AT_VALUE + C]).astype(BF16)
        return projected, inside

    projected, inside = tokens(s)
    base[...] = projected
    query[...] = mt(inside, wn[:, AT_QUERY : AT_QUERY + C]).astype(BF16)

    def others(d, _):
        tokens(lax.rem(s + d, 8))
        return 0

    lax.fori_loop(1, 8, others, 0)

    scale = math.log2(math.e) / math.sqrt(HEAD_SIZE)
    half = lax.broadcasted_iota(jnp.int32, (1, 128), 1) < 64

    def two_heads(p, _):
        lanes = pl.ds(pl.multiple_of(p * 128, 128), 128)
        mine = query[:, lanes]
        key_part = keys[:, lanes]
        value_part = values[:, lanes]
        results = []
        for keep in (half, jnp.logical_not(half)):
            one_query = jnp.where(keep, mine.astype(F32), 0.0).astype(BF16)
            scores = mt(one_query, key_part)
            top = jnp.max(scores, axis=1, keepdims=True)
            weights = jnp.exp2((scores - top) * scale)
            bottom = jnp.sum(weights, axis=1, keepdims=True)
            results.append(mm(weights.astype(BF16), value_part) / bottom)
        query[:, lanes] = jnp.where(half, results[0], results[1]).astype(BF16)
        return 0

    lax.fori_loop(0, 4, two_heads, 0)
    attended = mm(query[...], spread[...]).astype(BF16)
    mixture = (mt(attended, wn[:, AT_MIX : AT_MIX + C]) + base[...]).astype(BF16)
    mixture = mm(mixture, spread[...]).astype(BF16)
    outer = mt(mixture, wn[:, AT_OUTER : AT_OUTER + C])
    two = (block[...].astype(F32) + outer).astype(BF16)
    swap = exchange(1, two, two6)
    sums = exchanged(1, *swap)
    factor, shift = affine(sums, gwide[...], wide_vecs[7:8], EPS_BLOCK)
    into_taps(two6[...], factor, shift)
    out[...] = mt(taps[...], wout[...])

    for copy in pending:
        copy.wait_send()

    @pl.when(chip < 3)
    def _():
        first_up.wait_send()

    @pl.when(chip > 0)
    def _():
        first_dn.wait_send()

    for q in range(4):
        to_sib(q).wait_send()
    for h in range(1, 3):

        @pl.when((chip >= h) & (chip < 3))
        def _(h=h):
            ups(h)[1].wait_send()

        @pl.when((chip + h <= 3) & (chip > 0))
        def _(h=h):
            dns(h)[1].wait_send()


def run_block(piece, nt, wave, vecs, win, wout):
    dma = pltpu.SemaphoreType.DMA
    vmem = pl.BlockSpec(memory_space=pltpu.VMEM)
    return pl.pallas_call(
        block_kernel,
        out_shape=jax.ShapeDtypeStruct((OWN_TOKENS, 8), F32),
        in_specs=[vmem] * 6,
        out_specs=vmem,
        scratch_shapes=[
            pltpu.VMEM((CHUNKS, 64, 8, CHUNK), BF16),
            pltpu.VMEM((WIDE, CHUNKS * CHUNK), BF16),
            pltpu.VMEM((OWN_TOKENS, TAPS), BF16),
            pltpu.VMEM((2048 + 2 * ROW, 128), BF16),
            pltpu.VMEM((8, 16, OWN_TOKENS), BF16),
            pltpu.VMEM((EDGED, WIDE), BF16),
            pltpu.VMEM((EDGED, WIDE), BF16),
            pltpu.VMEM((EDGED, WIDE), BF16),
            pltpu.VMEM((OWN_TOKENS, WIDE), BF16),
            pltpu.VMEM((8, OWN_TOKENS, C), BF16),
            pltpu.VMEM((3, 8, 8, WIDE), F32),
            pltpu.VMEM((WIDE, C), BF16),
            pltpu.VMEM((WIDE, WIDE), BF16),
            pltpu.VMEM((C, C), BF16),
            pltpu.VMEM((2048, WIDE), BF16),
            pltpu.VMEM((2048, WIDE), BF16),
            pltpu.VMEM((OWN_TOKENS, WIDE), BF16),
            pltpu.VMEM((OWN_TOKENS, WIDE), F32),
            dma((OWN,)),
            dma((OWN,)),
            dma((OWN, 7)),
            dma((OWN, 7)),
            dma((OWN, 3)),
            dma((OWN, 3)),
            dma((OWN, 4)),
            dma((OWN, 4)),
            dma((7,)),
            dma((7,)),
            dma((3, 7)),
            dma((3, 7)),
            dma((2, 2)),
            dma((2, 2)),
            dma((3,)),
            dma((3,)),
            dma((3,)),
            dma((3,)),
            dma((4,)),
            dma((4,)),
        ],
        compiler_params=pltpu.CompilerParams(
            collective_id=0, has_side_effects=True, vmem_limit_bytes=58 << 20
        ),
        name="unet_level",
    )(piece, nt, wave, vecs, win, wout)


def body(
    latents,
    noise_draw,
    timesteps,
    inlet_conv,
    time_first,
    time_first_bias,
    time_second,
    time_second_bias,
    conv_first,
    conv_second,
    proj_inner,
    query_weight,
    key_weight,
    value_weight,
    attn_out,
    proj_outer,
    outlet_conv,
    first_gain,
    second_gain,
    third_gain,
    final_gain,
    layer_gain,
):
    piece = piece_of(
        time_first,
        time_second,
        (conv_first, conv_second),
        (proj_inner, query_weight, key_weight, value_weight, attn_out, proj_outer),
    )
    alpha_bar = lookup(timesteps)[:, None, None, None]
    noisy = (jnp.sqrt(alpha_bar) * latents + jnp.sqrt(1.0 - alpha_bar) * noise_draw).astype(BF16)
    padded = jnp.pad(noisy[0], ((0, 0), (1, 1), (0, 0)))
    turned = padded.transpose(2, 0, 1)
    nt = jnp.concatenate([turned[:, :, dx : dx + ROW] for dx in range(3)], axis=0).reshape(12, OWN_TOKENS)
    nt = jnp.pad(nt, ((0, 4), (0, 0)))
    wave = jnp.broadcast_to(waveform_of(timesteps, C // 2), (8, C))
    bias_one = time_first_bias.reshape(64, 4, 5).transpose(1, 0, 2).reshape(4, C)
    vecs = jnp.concatenate(
        [
            bias_one,
            jnp.stack([time_second_bias, first_gain, second_gain, final_gain, layer_gain, third_gain]),
            jnp.zeros((6, C), F32),
        ],
        axis=0,
    )
    win = jnp.pad(inlet_conv.reshape(3, 12, C), ((0, 0), (0, 4), (0, 0))).reshape(48, C)
    win = jnp.pad(win, ((0, 80), (0, 0)))
    wout = jnp.pad(outlet_conv.T, ((0, 4), (0, TAPS - 9 * C)))
    predicted = run_block(piece, nt, wave, vecs, win, wout)
    predicted = predicted[:, :4].reshape(noise_draw.shape)
    return (1.0 - alpha_bar) * (predicted - noise_draw)


def solution(mesh):
    in_specs = (
        P("batch", "space", None, None),
        P("batch", "space", None, None),
        P("batch"),
        P(),
        P(None, "batch"),
        P(),
        P(None, "batch"),
        P(),
        P(None, "batch"),
        P(None, "batch"),
        P(None, "batch"),
        P(None, "batch"),
        P(None, "batch"),
        P(None, "batch"),
        P(None, "batch"),
        P(None, "batch"),
        P(),
        P(),
        P(),
        P(),
        P(),
        P(),
    )
    out_specs = P("batch", "space", None, None)
    return jax.shard_map(body, mesh=mesh, in_specs=in_specs, out_specs=out_specs, check_vma=False)
```

time: 297 us -> 169 us (0.57)
  Pallas kernels: 91.7 us -> 147 us
  waiting for transfers between devices: 45.3 us -> 0 us
  matrix products: 34.4 us -> 0 us
  local copies, waits for them, and re-layouts: 45.8 us -> 17.8 us
  starting transfers between devices: 27.7 us -> 0 us
  blocking collectives: 23.8 us -> 0 us
  between operations: 16.4 us -> 2.25 us
  other arithmetic: 10.4 us -> 1.76 us
    pallas_call x1, Pallas kernels: 91.7 us -> 147 us  [run_block(): pl.pallas_call(block_kernel, out_shape=jax.ShapeDtypeStruct((OWN_TOKENS,...]
    all_gather x1 -> x0, waiting for transfers between devices: 37.9 us -> none  [in_one_piece(): filled = lax.all_gather(both, axis, axis=dim, tiled=True)]
    dot_general x52 -> x0, matrix products: 34.4 us -> none  [the longest x36 17.9 us: convolve(): jnp.einsum('bhwc,cd->bhwd', window, kernel[offset * width_in:(offset + 1)...]
    ppermute x8 -> x0, starting transfers between devices: 24.3 us -> none  [the longest x4 12.9 us: extended(): lax.ppermute(tail, axis, [(i, (i + 1) % count) for i in range(ends)])]
    all_to_all x3 -> x0, blocking collectives: 23.8 us -> none  [from_everyone(): lax.all_to_all(jnp.broadcast_to(shard[None], (length, *shard.shape)), axi...]
    reshape x10 -> x9, local copies, waits for them, and re-layouts: 19.5 us -> 2.49 us  [the longest x1 1 us: body(): predicted = predicted[:, :4].reshape(noise_draw.shape)]
    reduce_sum x17 -> x0, other arithmetic: 6.11 us -> none  [the longest x4 5.05 us: keys_everywhere(): row_sum = row_sum * shrink + jnp.sum(weights, axis=-1)]
    unnamed x45 -> x53, local copies, waits for them, and re-layouts: 16.2 us -> 10.4 us
  transfers between devices with their start and end apart: 10 -> 0, of which waited for: 4 -> 0; matrix products, arithmetic and copies ran while one was open for 13% -> 0% of each run, Pallas kernels for 31% -> 0%
where the time goes in v2:
time: 169 us; the launch traced here: 168 us
  Pallas kernels  147 us (87%)
  local copies, waits for them, and re-layouts  17.8 us (11%)
  between operations  2.25 us (1%)
  other arithmetic  1.76 us (1%)
    pallas_call x1, Pallas kernels, run_block(): pl.pallas_call(block_kernel, out_shape=jax.ShapeDtypeStruct((OWN_TOKENS,...  147 us
    unnamed x53, local copies, waits for them, and re-layouts  10.4 us

profile of v2, /device:TPU:1, one launch (start us, length us, event | category | flops | bytes accessed | tf_op | source)
XLA Modules:
  0.0 168.5 jit_solution(5518932110126175005)
XLA Ops:
  1.3 0.6 select_reduce_fusion
  3.6 0.6 pad.73.nt
  4.3 0.6 broadcast_in_dim.9.wave
  6.0 0.7 copy-done.6
  6.8 0.8 copy-done
  7.6 0.8 copy-done.1
  8.4 0.7 copy-done.9
  9.0 0.7 copy-done.10
  9.7 0.7 copy-done.11
  10.4 0.7 copy-done.12
  11.1 0.7 copy-done.13
  11.8 0.7 copy-done.14
  12.5 0.7 pad.71
  14.2 0.7 copy-done.16
  14.9 0.7 copy-done.17
  15.5 0.7 copy-done.18
  16.2 0.7 copy-done.19
  16.9 0.7 copy-done.20
  17.6 1.2 concatenate.21.vecs
  18.9 0.7 pad.75.win
  19.6 0.6 pad.76.wout
  20.2 146.6 %unet_level.1 = f32[256,8]{1,0:T(8,128)} custom-call(bf16[8,8,1408]{2,1,0:T(8,128)(2,1)} %bitcast.41, bf16[16,256]{1,0:T(8,128)(2,1)} %pad.73.nt, bf16[8,320]{1,0:T(8,128)(2,1)} %broadcast_in_dim.9.wave, f32[16,320]{1,0:T(8,128)} %concatenate.21.vecs, bf16[128,320]{1,0:T(8,128)(2,1)} %pad.75.win, bf16[8,2944]{1,0:T(8,128)(2,1)} %pad.76.wout), custom_call_target="tpu_custom_call" | custom-call | tf_op jit(solution)/shard_map/unet_level/pallas_call | solution.py:553
  166.8 1.0 copy.30
  167.8 0.6 subtract_multiply_fusion
  (72 shorter events, 3.3 us)
Async XLA Ops:
  0.5 2.7 %copy-start.8 = (f32[1,4,64,4]{2,3,1,0:T(4,128)S(1)}, f32[1,4,64,4]{2,3,1,0:T(4,128)}, u32[]{:S(2)}) copy-start(f32[1,4,64,4]{2,3,1,0:T(4,128)} %param.22) | copy-start | bytes 12292
  0.6 2.7 %copy-start.2 = (f32[1,4,64,4]{2,3,1,0:T(4,128)S(1)}, f32[1,4,64,4]{2,3,1,0:T(4,128)}, u32[]{:S(2)}) copy-start(f32[1,4,64,4]{2,3,1,0:T(4,128)} %param.23) | copy-start | bytes 12292
  3.6 1.3 copy-start.5
  6.0 0.7 copy-start.6
  6.7 0.8 copy-start
  7.5 0.8 copy-start.1
  8.3 0.7 copy-start.9
  9.0 0.7 copy-start.10
  9.7 0.7 copy-start.11
  10.4 0.7 copy-start.12
  11.1 0.7 copy-start.13
  11.8 0.7 copy-start.14
  12.5 0.7 copy-start.7
  13.5 0.7 copy-start.15
  14.2 0.7 copy-start.16
  14.8 0.7 copy-start.17
  15.5 0.7 copy-start.18
  16.2 0.7 copy-start.19
  16.9 0.7 copy-start.20
  17.6 1.2 copy-start.3
  18.8 0.7 copy-start.4

commit v3 on v2

--- a/solution.py
+++ b/solution.py
@@ -18,58 +18,25 @@
 EPS_LAYER = 1e-05
 
 
-def plan():
-    fraction = jnp.arange(STEPS, dtype=jnp.float32) / (STEPS - 1)
-    beta_root = math.sqrt(0.00085) + fraction * (math.sqrt(0.012) - math.sqrt(0.00085))
-    return jnp.cumprod(1.0 - beta_root * beta_root)
-
-
-def lookup(timesteps):
-    plan_tab = plan()
-    matches = jnp.arange(STEPS, dtype=jnp.int32)[None, :] == timesteps[:, None]
-    return jnp.sum(jnp.where(matches, plan_tab[None, :], 0.0), axis=1)
-
-
-def waveform_of(timesteps, halfway):
-    frequency = jnp.exp(-math.log(10000.0) * jnp.arange(halfway, dtype=jnp.float32) / halfway)
-    angles = timesteps.astype(jnp.float32)[:, None] * frequency[None, :]
-    return jnp.concatenate([jnp.cos(angles), jnp.sin(angles)], axis=1).astype(jnp.bfloat16)
-
-
 C = 320
 WIDE = 512
 ROW = 64
 OWN_TOKENS = 256
 EDGED = OWN_TOKENS + 2 * ROW
 TAPS = 2944
-CHUNKS = 8
-CHUNK = 1408
-OWN = CHUNKS // 2
-AT_FIRST = 0
-AT_SECOND = 1536
-AT_CONV_ONE = 3072
-AT_CONV_TWO = 6016
-AT_INNER, AT_QUERY, AT_KEY, AT_VALUE, AT_MIX, AT_OUTER = (8960 + 384 * i for i in range(6))
+LENGTHS = (1408, 1408, 1280, 1280)
+BASES = (0, 2816, 5632, 8192)
+LANES = 10752
+OWN = 4
+AT_SECOND = 1280
+AT_CONV_ONE = 2560
+AT_CONV_TWO = 5504
+AT_INNER, AT_QUERY, AT_KEY, AT_VALUE, AT_MIX, AT_OUTER = (8448 + 384 * i for i in range(6))
 MESH = pl.DeviceIdType.MESH
 F32 = jnp.float32
 BF16 = jnp.bfloat16
 
 
-def widened(turned, width):
-    return jnp.pad(turned, ((0, 0), (0, width - turned.shape[1])))
-
-
-def piece_of(first, second, convs, squares):
-    tf = first.T.reshape(4, 5, C).transpose(1, 0, 2)
-    tf = jnp.pad(tf, ((0, 0), (0, 0), (0, 64))).reshape(5, 1536)
-    ts = second.T.reshape(5, 64, 4, 5).transpose(0, 2, 1, 3).reshape(5, 4, C)
-    ts = jnp.pad(ts, ((0, 0), (0, 0), (0, 64))).reshape(5, 1536)
-    rows = [tf, ts] + [widened(c.T, TAPS) for c in convs] + [widened(m.T, 384) for m in squares]
-    rows = jnp.concatenate(rows, axis=1)
-    rows = jnp.pad(rows, ((0, 3), (0, 0)))
-    return rows.reshape(8, CHUNKS, CHUNK).transpose(1, 0, 2)
-
-
 def mm(a, b):
     return lax.dot_general(a, b, (((1,), (0,)), ((), ())), preferred_element_type=F32)
 
@@ -79,11 +46,12 @@
 
 
 def exactly(product, v, matrix):
-    high = v.astype(BF16)
-    rest = v - high.astype(F32)
-    mid = rest.astype(BF16)
-    low = (rest - mid.astype(F32)).astype(BF16)
-    return product(high, matrix) + product(mid, matrix) + product(low, matrix)
+    count = v.shape[0]
+    high = v.astype(BF16).astype(F32)
+    mid = (v - high).astype(BF16).astype(F32)
+    low = v - high - mid
+    parts = product(jnp.concatenate([high, mid, low], axis=0).astype(BF16), matrix)
+    return parts[:count] + parts[count : 2 * count] + parts[2 * count :]
 
 
 def silu(v):
@@ -91,53 +59,57 @@
     return half + half * jnp.tanh(half)
 
 
-def block_kernel(
-    piece,
-    nt,
-    wave,
-    vecs,
-    win,
-    wout,
-    out,
-    w,
-    wn,
-    taps,
-    xt,
-    nview,
-    start,
-    mid6,
-    two6,
-    block,
-    nat,
-    stats,
-    spread,
-    gwide,
-    gslim,
-    keys,
-    values,
-    query,
-    base,
-    y_s,
-    y_r,
-    z_s,
-    z_r,
-    x_s,
-    x_r,
-    c_s,
-    c_r,
-    n_s,
-    n_r,
-    t_s,
-    t_r,
-    h_s,
-    h_r,
-    up_s,
-    up_r,
-    dn_s,
-    dn_r,
-    k_s,
-    k_r,
-):
+def block_kernel(step, *refs):
+    sources = refs[:21]
+    out = refs[21]
+    held = refs[22:43]
+    (
+        w0,
+        w1,
+        w2,
+        w3,
+        wn,
+        flat,
+        taps,
+        xt,
+        nt,
+        nview,
+        start,
+        mid6,
+        two6,
+        block,
+        nat,
+        stats,
+        spread,
+        gwide,
+        gslim,
+        keys,
+        values,
+        query,
+        base,
+        l_s,
+        y_s,
+        y_r,
+        a_s,
+        a_r,
+        b_s,
+        b_r,
+        c_s,
+        c_r,
+        n_s,
+        n_r,
+        t_s,
+        t_r,
+        h_s,
+        h_r,
+        up_s,
+        up_r,
+        dn_s,
+        dn_r,
+        k_s,
+        k_r,
+    ) = refs[43:]
+    w = (w0, w1, w2, w3)
     b = lax.axis_index("batch")
     s = lax.axis_index("space")
     yh = lax.rem(b, 2)
@@ -148,26 +120,62 @@
     sib = s + 1 - 2 * core
     mate = b + 1 - 2 * yh
 
-    def at_z(zz):
-        return (x * 8 + zz) * 2 + yh
-
-    def at_x(xx):
-        return (xx * 8 + z) * 2 + yh
-
-    zs = [lax.rem(z + d, 8) for d in range(8)]
-    xs = [lax.rem(x + d, 4) for d in range(4)]
-    x_from = [lax.rem(x + 4 - d, 4) for d in range(4)]
+    loads = [pltpu.make_async_copy(h, v, l_s.at[i]) for i, (h, v) in enumerate(zip(sources, held))]
+    for load in loads:
+        load.start()
+
+    def at_z(d):
+        return ((x * 8 + lax.rem(z + d, 8)) * 2 + yh, s)
+
+    def at_x(d):
+        return ((lax.rem(x + d, 4) * 8 + z) * 2 + yh, s)
+
     peers = [lax.rem(s + d, 8) for d in range(8)]
-    peers_from = [lax.rem(s + 8 - d, 8) for d in range(8)]
-
     barrier = pltpu.get_barrier_semaphore()
-    friends = [(mate, s)] + [(at_z(q), s) for q in zs[1:]] + [(at_x(q), s) for q in xs[1:]]
+    friends = [(mate, 2 * q + core) for q in range(4)] + [at_z(1), at_z(7), at_x(1), at_x(3)]
     friends += [(b, q) for q in peers[1:]]
     for dev in friends:
         pl.semaphore_signal(barrier, inc=1, device_id=dev, device_id_type=MESH)
+    for load in loads:
+        load.wait()
+    field8, wave, first, second, conv_a, conv_b = held[:6]
+    squares = held[6:12]
+    inlet, outlet, bias_a = held[12:15]
+    third = held[20]
+
+    def eight(rows):
+        rows = rows.astype(F32)
+        return jnp.concatenate([rows, jnp.zeros((8 - rows.shape[0], rows.shape[1]), F32)], axis=0).astype(BF16)
+
+    flat[...] = jnp.zeros((8, LANES), BF16)
+    turned = first[...].astype(F32)
+    for i in range(4):
+        flat[:, C * i : C * i + C] = eight(turned[5 * i : 5 * i + 5])
+    flat[:, AT_SECOND : AT_SECOND + 1280] = eight(second[...])
+    flat[:, AT_CONV_ONE : AT_CONV_ONE + 9 * C] = eight(conv_a[...])
+    flat[:, AT_CONV_TWO : AT_CONV_TWO + 9 * C] = eight(conv_b[...])
+    for i in range(6):
+        flat[:, AT_INNER + 384 * i : AT_INNER + 384 * i + C] = eight(squares[i][...])
+
+    place = lax.broadcasted_iota(jnp.int32, (8, 128), 0) * 128 + lax.broadcasted_iota(jnp.int32, (8, 128), 1)
+    root = math.sqrt(0.00085) + place.astype(F32) / (STEPS - 1) * (math.sqrt(0.012) - math.sqrt(0.00085))
+    abar = jnp.where(place <= step[0], 1.0 - root * root, 1.0)
+    for shift in (1, 2, 4, 8, 16, 32, 64):
+        abar = abar * pltpu.roll(abar, shift, 1)
+    for shift in (1, 2, 4):
+        abar = abar * pltpu.roll(abar, shift, 0)
+    abar = abar[0:1, 0:1]
+    noisy = jnp.sqrt(abar) * field8[0:4, :] + jnp.sqrt(1.0 - abar) * field8[4:8, :]
+    noisy = noisy.astype(BF16).astype(F32)
+    place = lax.bitwise_and(lax.broadcasted_iota(jnp.int32, (4, OWN_TOKENS), 1), ROW - 1)
+    west = jnp.where(place == 0, 0.0, pltpu.roll(noisy, 1, 1))
+    east = jnp.where(place == ROW - 1, 0.0, pltpu.roll(noisy, OWN_TOKENS - 1, 1))
+    shifted = jnp.concatenate([west, noisy, east, jnp.zeros((4, OWN_TOKENS), F32)], axis=0).astype(BF16)
+    nt[...] = shifted
+    nview[s] = shifted
+    own = [pl.ds(pl.multiple_of(BASES[i] + core * LENGTHS[i], 128), LENGTHS[i]) for i in range(OWN)]
     for i in range(OWN):
-        w[2 * i + core, b] = piece[2 * i + core]
-    nview[s] = nt[...]
+        w[i][core, x, z, yh] = flat[:, own[i]]
     pl.semaphore_wait(barrier, len(friends))
 
     def send(src, dst, ss, rs, dev):
@@ -176,19 +184,125 @@
         )
 
     pending = []
-    ys, zc, xc, cc = [], {}, {}, {}
+
+    def go(copy):
+        copy.start()
+        pending.append(copy)
+        return copy
+
+    def crossing(i, k, to):
+        return send(flat.at[:, own[i]], w[i].at[core, x, z, yh], y_s.at[i, k], y_r.at[i], (mate, 2 * to + core))
+
     for i in range(OWN):
-        c = 2 * i + core
-        copy = send(piece.at[c], w.at[c, b], y_s.at[i], y_r.at[i], (mate, s))
-        copy.start()
-        ys.append(copy)
-        pending.append(copy)
+        for k in range(2):
+
+            @pl.when(chip == 0)
+            def _(i=i, k=k):
+                crossing(i, k, 3 - k).start()
+
+            @pl.when(chip == 3)
+            def _(i=i, k=k):
+                crossing(i, k, k).start()
+
     ns = []
     for d in range(1, 8):
-        copy = send(nt, nview.at[s], n_s.at[d - 1], n_r.at[d - 1], (b, peers[d]))
-        copy.start()
-        ns.append(copy)
-        pending.append(copy)
+        ns.append(go(send(nt, nview.at[s], n_s.at[d - 1], n_r.at[d - 1], (b, peers[d]))))
+
+    def z_ring(i, view, half):
+        def block(d):
+            return view(lax.rem(z + 8 + d, 8))
+
+        def copies(t):
+            if t < 3:
+                one, two = block(-t), block(t)
+            else:
+                one, two = half(lax.rem(z + 8 - t, 8), 0), half(lax.rem(z + t, 8), 1)
+            return (
+                send(one, one, a_s.at[i, 2 * t], a_r.at[i, 2 * t], at_z(1)),
+                send(two, two, a_s.at[i, 2 * t + 1], a_r.at[i, 2 * t + 1], at_z(7)),
+            )
+
+        def landed(t):
+            if t < 3:
+                return block(-1 - t), block(1 + t)
+            return half(lax.rem(z + 4, 8), 0), half(lax.rem(z + 4, 8), 1)
+
+        return 4, copies, landed
+
+    def x_ring(i, view, half):
+        def block(d):
+            return view(lax.rem(x + 4 + d, 4))
+
+        def copies(t):
+            if t < 1:
+                one, two = block(0), block(0)
+            else:
+                one, two = half(lax.rem(x + 3, 4), 0), half(lax.rem(x + 1, 4), 1)
+            return (
+                send(one, one, b_s.at[i, 2 * t], b_r.at[i, 2 * t], at_x(1)),
+                send(two, two, b_s.at[i, 2 * t + 1], b_r.at[i, 2 * t + 1], at_x(3)),
+            )
+
+        def landed(t):
+            if t < 1:
+                return block(-1), block(1)
+            return half(lax.rem(x + 2, 4), 0), half(lax.rem(x + 2, 4), 1)
+
+        return 2, copies, landed
+
+    def rings(i, k):
+        wk = w[i].at[k]
+        if i % 2 == 0:
+            small = z_ring(i, lambda q: wk.at[x, q], lambda q, h: wk.at[x, q, h])
+            large = x_ring(i, lambda q: wk.at[q], lambda q, h: wk.at[q, pl.ds(4 * h, 4)])
+            mine = wk.at[x]
+        else:
+            small = x_ring(i, lambda q: wk.at[q, z], lambda q, h: wk.at[q, z, h])
+            large = z_ring(i, lambda q: wk.at[:, q], lambda q, h: wk.at[pl.ds(2 * h, 2), q])
+            mine = wk.at[:, z]
+        return small, large, mine
+
+    mine_rings = [rings(i, core) for i in range(OWN)]
+    theirs = [rings(i, 1 - core) for i in range(OWN)]
+    flying = {}
+
+    def launch(i, which, t):
+        flying[i, which, t] = [go(copy) for copy in mine_rings[i][which][1](t)]
+
+    def to_sib(i, j, ref):
+        go(send(ref, ref, c_s.at[i, j], c_r.at[i, j], (b, sib)))
+
+    def land(i, which, t):
+        count, _, landed = mine_rings[i][which]
+        for copy in flying[i, which, t]:
+            copy.wait_recv()
+        if t + 1 < count:
+            launch(i, which, t + 1)
+        elif which == 0:
+            launch(i, 1, 0)
+            to_sib(i, 0, mine_rings[i][2])
+        if which == 1:
+            for j, ref in enumerate(landed(t)):
+                to_sib(i, 1 + 2 * t + j, ref)
+
+    def cross(i):
+        send(flat.at[:, own[i]], w[i].at[core, x, z, 1 - yh], y_s.at[i, 0], y_r.at[i], (mate, s)).wait_recv()
+        launch(i, 0, 0)
+
+    def unpack(i):
+        count, _, landed = theirs[i][1]
+        refs = [theirs[i][2]] + [ref for t in range(count) for ref in landed(t)]
+        for j, ref in enumerate(refs):
+            send(ref, ref, c_s.at[i, j], c_r.at[i, j], (b, sib)).wait_recv()
+
+        def two(p, _):
+            for k in range(2):
+                both = w[i][k, lax.div(p, 8), lax.rem(p, 8)].astype(F32).reshape(16, LENGTHS[i])
+                at = BASES[i] + k * LENGTHS[i]
+                wn[pl.ds(pl.multiple_of(p * 16, 16), 16), at : at + LENGTHS[i]] = both.astype(BF16)
+            return 0
+
+        lax.fori_loop(0, 32, two, 0)
 
     wide_i = lax.broadcasted_iota(jnp.int32, (WIDE, C), 0)
     slim_j = lax.broadcasted_iota(jnp.int32, (WIDE, C), 1)
@@ -196,6 +310,8 @@
         lax.bitwise_and(wide_i, 7) < 5
     )
     spread[...] = jnp.where(hit, 1.0, 0.0).astype(BF16)
+    cross(0)
+    cross(1)
     gi = lax.broadcasted_iota(jnp.int32, (WIDE, WIDE), 0)
     gj = lax.broadcasted_iota(jnp.int32, (WIDE, WIDE), 1)
     same = lax.shift_right_logical(gi, 4) == lax.shift_right_logical(gj, 4)
@@ -204,8 +320,14 @@
     nj = lax.broadcasted_iota(jnp.int32, (C, C), 1)
     apart = ni - lax.div(nj, 10) * 10
     gslim[...] = jnp.where((apart >= 0) & (apart < 10), 1.0, 0.0).astype(BF16)
-    wide_vecs = exactly(mt, vecs[...], spread[...])
-    win_wide = mt(win[...], spread[...]).astype(BF16)
+    vecs = jnp.concatenate([v[...] for v in held[15:20]] + [jnp.zeros((3, C), F32)], axis=0)
+    wide_vecs = exactly(mt, vecs, spread[...])
+    taken = inlet[...].astype(F32)
+    taken = [jnp.concatenate([taken[12 * q : 12 * q + 12], jnp.zeros((4, C), F32)], axis=0) for q in range(3)]
+    win = jnp.concatenate(taken + [jnp.zeros((80, C), F32)], axis=0).astype(BF16)
+    win_wide = mt(win, spread[...]).astype(BF16)
+    land(1, 0, 0)
+    land(0, 0, 0)
 
     for copy in ns:
         copy.wait_recv()
@@ -218,16 +340,12 @@
     xt[ROW + 2048 : 2 * ROW + 2048, :] = jnp.zeros((ROW, 128), BF16)
     xt[ROW : ROW + 2048, :] = rows.T.astype(BF16)
 
-    pair = b - yh
-    for i in range(OWN):
-        c = 2 * i + core
-        ys[i].wait_recv()
-        for d in range(1, 8):
-            part = w.at[c, pl.ds(pair, 2)]
-            copy = send(part, part, z_s.at[i, d - 1], z_r.at[i, d - 1], (at_z(zs[d]), s))
-            copy.start()
-            zc[i, d] = copy
-            pending.append(copy)
+    land(1, 0, 1)
+    land(0, 0, 1)
+    land(0, 0, 2)
+    land(0, 0, 3)
+    cross(2)
+    cross(3)
 
     def start_sums(q, carry):
         total, squared = carry
@@ -263,59 +381,41 @@
                 tap = 3 * dy + dx
                 taps[:, tap * C : (tap + 1) * C] = shifted[dy * ROW : dy * ROW + OWN_TOKENS]
 
-    for i in range(OWN):
-        c = 2 * i + core
-        for d in range(1, 8):
-            zc[i, d].wait_recv()
-        part = w.at[c, pl.ds(x * 16, 16)]
-        for d in range(1, 4):
-            copy = send(part, part, x_s.at[i, d - 1], x_r.at[i, d - 1], (at_x(xs[d]), s))
-            copy.start()
-            xc[i, d] = copy
-            pending.append(copy)
-        copy = send(part, part, c_s.at[i, 0], c_r.at[i, 0], (b, sib))
-        copy.start()
-        cc[i, 0] = copy
-        pending.append(copy)
-
+    land(1, 1, 0)
+    land(2, 0, 0)
+    land(3, 0, 0)
     taps[:, 9 * C :] = jnp.zeros((OWN_TOKENS, TAPS - 9 * C), BF16)
-    factor, shift = affine(stacked(total, squared), gwide[...], wide_vecs[5:6], EPS_BLOCK)
+    factor, shift = affine(stacked(total, squared), gwide[...], wide_vecs[0:1], EPS_BLOCK)
     into_taps(start[...], factor, shift)
 
-    def arrive(i):
-        c = 2 * i + core
-        for d in range(1, 4):
-            xc[i, d].wait_recv()
-            part = w.at[c, pl.ds(x_from[d] * 16, 16)]
-            copy = send(part, part, c_s.at[i, d], c_r.at[i, d], (b, sib))
-            copy.start()
-            cc[i, d] = copy
-            pending.append(copy)
-
-    def unpack(i):
-        for d in range(4):
-            cc[i, d].wait_recv()
-
-        def two(p, _):
-            for c in (2 * i, 2 * i + 1):
-                both = w[c, pl.ds(2 * p, 2)].astype(F32).reshape(16, CHUNK)
-                wn[pl.ds(pl.multiple_of(p * 16, 16), 16), c * CHUNK : (c + 1) * CHUNK] = both.astype(BF16)
-            return 0
-
-        lax.fori_loop(0, 32, two, 0)
-
-    arrive(0)
-    arrive(1)
+    land(1, 1, 1)
+    land(0, 1, 0)
+    land(2, 0, 1)
+    land(3, 0, 1)
+    row_p = lax.broadcasted_iota(jnp.int32, (C, 1), 0)
+    target = 4 * row_p - 3 * lax.rem(row_p, 5)
+    unit = lax.broadcasted_iota(jnp.int32, (C, 1280), 1)
+    orders = [jnp.where(unit == target + 5 * i, 1.0, 0.0).astype(BF16) for i in range(4)]
+    bias_rows = jnp.broadcast_to(bias_a[...], (8, 1280))
+    biases = [exactly(mt, exactly(mt, bias_rows, orders[i]), spread[...]) for i in range(4)]
+    land(2, 0, 2)
+    land(1, 1, 2)
+    land(0, 1, 1)
     unpack(0)
+    land(2, 0, 3)
+    land(1, 1, 3)
     unpack(1)
-    embedded = wide_vecs[4:5]
+    waves = jnp.broadcast_to(wave[...], (8, C))
+    hidden = jnp.zeros((8, 1280), F32)
     for i in range(4):
-        inner = mt(wave[...], wn[:, AT_FIRST + 384 * i : AT_FIRST + 384 * i + C])
-        hidden = silu(silu(inner + wide_vecs[i : i + 1])).astype(BF16)
-        hidden = mm(hidden, spread[...]).astype(BF16)
-        embedded = embedded + mt(hidden, wn[:, AT_SECOND + 384 * i : AT_SECOND + 384 * i + C])[0:1]
-    arrive(2)
-    unpack(2)
+        blank = jnp.zeros((8, C), F32)
+        placed = jnp.concatenate([waves, blank] if i % 2 == 0 else [blank, waves], axis=1).astype(BF16)
+        first_at = 640 * (i // 2)
+        inner = mt(placed, wn[:, first_at : first_at + 640])
+        part = silu(silu(inner + biases[i])).astype(BF16)
+        hidden = hidden + mm(mm(part, spread[...]).astype(BF16), orders[i])
+    embedded = mt(hidden.astype(BF16), wn[:, AT_SECOND : AT_SECOND + 1280])[0:1] + wide_vecs[4:5]
+    land(3, 1, 0)
     middle = (mt(taps[...], wn[:, AT_CONV_ONE : AT_CONV_ONE + TAPS]) + embedded).astype(BF16)
 
     def exchange(layer, field, edged):
@@ -383,11 +483,16 @@
         return gather_stats(layer, copies)
 
     swap = exchange(0, middle, mid6)
-    arrive(3)
+    land(2, 1, 0)
+    land(3, 1, 1)
+    sums = exchanged(0, *swap)
+    factor, shift = affine(sums, gwide[...], wide_vecs[1:2], EPS_BLOCK)
+    into_taps(mid6[...], factor, shift)
+    land(3, 1, 2)
+    land(2, 1, 1)
+    unpack(2)
+    land(3, 1, 3)
     unpack(3)
-    sums = exchanged(0, *swap)
-    factor, shift = affine(sums, gwide[...], wide_vecs[6:7], EPS_BLOCK)
-    into_taps(mid6[...], factor, shift)
     one = mt(taps[...], wn[:, AT_CONV_TWO : AT_CONV_TWO + TAPS])
     one = (one + start[ROW : ROW + OWN_TOKENS, :].astype(F32)).astype(BF16)
     block[...] = one
@@ -406,7 +511,7 @@
     def hop(source, towards, ss, rs):
         return send(nat.at[source], nat.at[source], ss, rs, (b, towards))
 
-    def to_sib(source_chip):
+    def kin(source_chip):
         source = 2 * source_chip + core
         return hop(source, sib, k_s.at[source_chip], k_r.at[source_chip])
 
@@ -421,7 +526,7 @@
     def _():
         first_dn.start()
 
-    to_sib(chip).start()
+    kin(chip).start()
 
     def ups(h):
         source = s - 2 * h
@@ -447,7 +552,7 @@
                 def _():
                     on.start()
 
-            to_sib(chip - h).start()
+            kin(chip - h).start()
 
         @pl.when(chip + h <= 3)
         def _(h=h):
@@ -459,13 +564,13 @@
                 def _():
                     on.start()
 
-            to_sib(chip + h).start()
+            kin(chip + h).start()
 
     for q in range(4):
         source = 2 * q + 1 - core
         hop(source, sib, k_s.at[q], k_r.at[q]).wait_recv()
     sums = gather_stats(2, copies)
-    factor, shift = affine(sums[:, :C], gslim[...], vecs[9:10, :], EPS_GROUP)
+    factor, shift = affine(sums[:, :C], gslim[...], third[...], EPS_GROUP)
     lane = lax.broadcasted_iota(jnp.int32, (1, WIDE), 1)
     real = lax.bitwise_and(lane, 7) < 5
 
@@ -475,7 +580,7 @@
         mean = jnp.sum(projected, axis=1, keepdims=True) * (1.0 / C)
         centred = jnp.where(real, projected - mean, 0.0)
         spreadness = jnp.sum(centred * centred, axis=1, keepdims=True) * (1.0 / C)
-        inside = (centred * lax.rsqrt(spreadness + EPS_LAYER) * wide_vecs[8:9]).astype(BF16)
+        inside = (centred * lax.rsqrt(spreadness + EPS_LAYER) * wide_vecs[3:4]).astype(BF16)
         inside = mm(inside, spread[...]).astype(BF16)
         where = pl.ds(pl.multiple_of(q * 256, 256), 256)
         keys[where, :] = mt(inside, wn[:, AT_KEY : AT_KEY + C]).astype(BF16)
@@ -519,9 +624,24 @@
     two = (block[...].astype(F32) + outer).astype(BF16)
     swap = exchange(1, two, two6)
     sums = exchanged(1, *swap)
-    factor, shift = affine(sums, gwide[...], wide_vecs[7:8], EPS_BLOCK)
+    factor, shift = affine(sums, gwide[...], wide_vecs[2:3], EPS_BLOCK)
     into_taps(two6[...], factor, shift)
-    out[...] = mt(taps[...], wout[...])
+    taken = outlet[...].astype(F32)
+    taken = jnp.concatenate([taken, jnp.zeros((4, 9 * C), F32)], axis=0)
+    taken = jnp.concatenate([taken, jnp.zeros((8, TAPS - 9 * C), F32)], axis=1).astype(BF16)
+    predicted = mt(taken, taps[...])
+    out[...] = (1.0 - abar) * (predicted[0:4] - field8[4:8, :])
+    for i in range(OWN):
+        for k in range(2):
+
+            @pl.when(chip == 0)
+            def _(i=i, k=k):
+                crossing(i, k, 3 - k).wait_send()
+
+            @pl.when(chip == 3)
+            def _(i=i, k=k):
+                crossing(i, k, k).wait_send()
+
 
     for copy in pending:
         copy.wait_send()
@@ -535,7 +655,7 @@
         first_dn.wait_send()
 
     for q in range(4):
-        to_sib(q).wait_send()
+        kin(q).wait_send()
     for h in range(1, 3):
 
         @pl.when((chip >= h) & (chip < 3))
@@ -547,19 +667,22 @@
             dns(h)[1].wait_send()
 
 
-def run_block(piece, nt, wave, vecs, win, wout):
+def run_block(step, sources):
     dma = pltpu.SemaphoreType.DMA
-    vmem = pl.BlockSpec(memory_space=pltpu.VMEM)
+    hbm = pl.BlockSpec(memory_space=pltpu.HBM)
     return pl.pallas_call(
         block_kernel,
-        out_shape=jax.ShapeDtypeStruct((OWN_TOKENS, 8), F32),
-        in_specs=[vmem] * 6,
-        out_specs=vmem,
-        scratch_shapes=[
-            pltpu.VMEM((CHUNKS, 64, 8, CHUNK), BF16),
-            pltpu.VMEM((WIDE, CHUNKS * CHUNK), BF16),
+        out_shape=jax.ShapeDtypeStruct((4, OWN_TOKENS), F32),
+        in_specs=[pl.BlockSpec(memory_space=pltpu.SMEM)] + [hbm] * len(sources),
+        out_specs=pl.BlockSpec(memory_space=pltpu.VMEM),
+        scratch_shapes=[pltpu.VMEM(a.shape, a.dtype) for a in sources]
+        + [pltpu.VMEM((2, 4, 8, 2, 8, length), BF16) for length in LENGTHS]
+        + [
+            pltpu.VMEM((WIDE, LANES), BF16),
+            pltpu.VMEM((8, LANES), BF16),
             pltpu.VMEM((OWN_TOKENS, TAPS), BF16),
             pltpu.VMEM((2048 + 2 * ROW, 128), BF16),
+            pltpu.VMEM((16, OWN_TOKENS), BF16),
             pltpu.VMEM((8, 16, OWN_TOKENS), BF16),
             pltpu.VMEM((EDGED, WIDE), BF16),
             pltpu.VMEM((EDGED, WIDE), BF16),
@@ -574,14 +697,15 @@
             pltpu.VMEM((2048, WIDE), BF16),
             pltpu.VMEM((OWN_TOKENS, WIDE), BF16),
             pltpu.VMEM((OWN_TOKENS, WIDE), F32),
+            dma((len(sources),)),
+            dma((OWN, 2)),
             dma((OWN,)),
-            dma((OWN,)),
-            dma((OWN, 7)),
-            dma((OWN, 7)),
-            dma((OWN, 3)),
-            dma((OWN, 3)),
+            dma((OWN, 8)),
+            dma((OWN, 8)),
             dma((OWN, 4)),
             dma((OWN, 4)),
+            dma((OWN, 9)),
+            dma((OWN, 9)),
             dma((7,)),
             dma((7,)),
             dma((3, 7)),
@@ -599,7 +723,7 @@
             collective_id=0, has_side_effects=True, vmem_limit_bytes=58 << 20
         ),
         name="unet_level",
-    )(piece, nt, wave, vecs, win, wout)
+    )(step, *sources)
 
 
 def body(
@@ -626,34 +750,31 @@
     final_gain,
     layer_gain,
 ):
-    piece = piece_of(
-        time_first,
-        time_second,
-        (conv_first, conv_second),
-        (proj_inner, query_weight, key_weight, value_weight, attn_out, proj_outer),
-    )
-    alpha_bar = lookup(timesteps)[:, None, None, None]
-    noisy = (jnp.sqrt(alpha_bar) * latents + jnp.sqrt(1.0 - alpha_bar) * noise_draw).astype(BF16)
-    padded = jnp.pad(noisy[0], ((0, 0), (1, 1), (0, 0)))
-    turned = padded.transpose(2, 0, 1)
-    nt = jnp.concatenate([turned[:, :, dx : dx + ROW] for dx in range(3)], axis=0).reshape(12, OWN_TOKENS)
-    nt = jnp.pad(nt, ((0, 4), (0, 0)))
-    wave = jnp.broadcast_to(waveform_of(timesteps, C // 2), (8, C))
-    bias_one = time_first_bias.reshape(64, 4, 5).transpose(1, 0, 2).reshape(4, C)
-    vecs = jnp.concatenate(
-        [
-            bias_one,
-            jnp.stack([time_second_bias, first_gain, second_gain, final_gain, layer_gain, third_gain]),
-            jnp.zeros((6, C), F32),
-        ],
-        axis=0,
-    )
-    win = jnp.pad(inlet_conv.reshape(3, 12, C), ((0, 0), (0, 4), (0, 0))).reshape(48, C)
-    win = jnp.pad(win, ((0, 80), (0, 0)))
-    wout = jnp.pad(outlet_conv.T, ((0, 4), (0, TAPS - 9 * C)))
-    predicted = run_block(piece, nt, wave, vecs, win, wout)
-    predicted = predicted[:, :4].reshape(noise_draw.shape)
-    return (1.0 - alpha_bar) * (predicted - noise_draw)
+    def turned(field):
+        return field[0].transpose(2, 0, 1).reshape(4, OWN_TOKENS)
+
+    halfway = C // 2
+    frequency = jnp.exp(-math.log(10000.0) * jnp.arange(halfway, dtype=F32) / halfway)
+    angles = timesteps.astype(F32)[:, None] * frequency[None, :]
+    wave = jnp.concatenate([jnp.cos(angles), jnp.sin(angles)], axis=1)
+    vectors = (first_gain, second_gain, final_gain, layer_gain, time_second_bias)
+    squares = (proj_inner, query_weight, key_weight, value_weight, attn_out, proj_outer)
+    sources = [
+        jnp.concatenate([turned(latents), turned(noise_draw)], axis=0),
+        wave,
+        time_first.T,
+        time_second.T,
+        conv_first.T,
+        conv_second.T,
+        *(m.T for m in squares),
+        inlet_conv,
+        outlet_conv.T,
+        time_first_bias.reshape(1, 4 * C),
+        *(v.reshape(1, C) for v in vectors),
+        third_gain.reshape(1, C),
+    ]
+    result = run_block(timesteps, sources)
+    return result.reshape(4, 4, ROW).transpose(1, 2, 0)[None]
 
 
 def solution(mesh):

time: 169 us -> 137 us (0.81)
  Pallas kernels: 147 us -> 128 us
  local copies, waits for them, and re-layouts: 17.8 us -> 6.94 us
    pallas_call x1, Pallas kernels: 147 us -> 128 us  [run_block(): pl.pallas_call(block_kernel, out_shape=jax.ShapeDtypeStruct((4, OWN_TOKEN...]
    unnamed x53 -> x18, local copies, waits for them, and re-layouts: 10.4 us -> 1.39 us
    reshape x9 -> x11, local copies, waits for them, and re-layouts: 2.49 us -> 5.55 us  [the longest x5 2.82 us: body(): v.reshape(1, C)]
    pad x6 -> x0, local copies, waits for them, and re-layouts: 2.62 us -> none  [the longest x1 0.7 us: piece_of(): rows = jnp.pad(rows, ((0, 3), (0, 0)))]
where the time goes in v3:
time: 137 us
  Pallas kernels  128 us (93%)
  local copies, waits for them, and re-layouts  6.94 us (5%)
    pallas_call x1, Pallas kernels, run_block(): pl.pallas_call(block_kernel, out_shape=jax.ShapeDtypeStruct((4, OWN_TOKEN...  128 us
    reshape x5, local copies, waits for them, and re-layouts, body(): v.reshape(1, C)  2.82 us

profile of v3, /device:TPU:1, one launch (start us, length us, event | category | flops | bytes accessed | tf_op | source)
XLA Modules:
  0.0 136.8 jit_solution(12766162770443333603)
XLA Ops:
  0.7 0.0 copy-start
  0.7 0.1 fusion
  0.7 0.6 pad_maximum_fusion.1.refs_1_
  1.4 0.1 reshape.56
  1.5 0.6 copy-done.1
  2.1 0.1 reshape.57
  2.2 0.6 pad_maximum_fusion.refs_0_
  2.8 0.1 copy-done.2
  2.9 0.6 reshape.58.refs_14_
  3.5 0.1 copy-done.3
  3.6 0.6 reshape.59.refs_15_
  4.1 0.1 copy-done.4
  4.2 0.6 reshape.60.refs_16_
  4.8 0.1 copy-done.5
  4.9 0.5 reshape.61.refs_17_
  5.5 0.1 copy-done.6
  5.6 0.6 reshape.62.refs_18_
  6.2 0.1 copy-done.7
  6.3 0.6 reshape.63.refs_19_
  6.9 0.1 copy-done.8
  7.0 0.6 reshape.64.refs_20_
  7.6 127.8 %unet_level.1 = f32[4,256]{1,0:T(4,128)} custom-call(s32[1]{0:T(128)S(6)} %copy.28.step, f32[8,256]{1,0:T(8,128)} %pad_maximum_fusion.refs_0_, f32[1,320]{1,0:T(1,128)} %pad_maximum_fusion.1.refs_1_, bf16[20,320]{1,0:T(8,128)(2,1)} %bitcast.27, bf16[5,1280]{1,0:T(8,128)(2,1)} %bitcast.26, bf16[5,2880]{1,0:T(8,128)(2,1)} %bitcast.23, ...), custom_call_target="tpu_custom_call" | custom-call | tf_op jit(solution)/shard_map/unet_level/pallas_call | solution.py:673
  135.4 0.8 reshape.65
  136.2 0.6 copy.27
  (11 shorter events, 0.0 us)
Async XLA Ops:
  0.7 0.7 copy-start
  1.4 0.7 copy-start.1
  2.2 0.7 copy-start.2
  2.9 0.7 copy-start.3
  3.6 0.7 copy-start.4
  4.2 0.7 copy-start.5
  4.9 0.7 copy-start.6
  5.6 0.7 copy-start.7
  6.3 0.7 copy-start.8

commit v4 on v3

--- a/solution.py
+++ b/solution.py
@@ -132,8 +132,8 @@
 
     peers = [lax.rem(s + d, 8) for d in range(8)]
     barrier = pltpu.get_barrier_semaphore()
-    friends = [(mate, 2 * q + core) for q in range(4)] + [at_z(1), at_z(7), at_x(1), at_x(3)]
-    friends += [(b, q) for q in peers[1:]]
+    edge = jnp.where(chip >= 2, core, 6 + core)
+    friends = [(mate, edge), at_z(1), at_z(7), at_x(1), at_x(3)] + [(b, q) for q in peers[1:]]
     for dev in friends:
         pl.semaphore_signal(barrier, inc=1, device_id=dev, device_id_type=MESH)
     for load in loads:
@@ -156,6 +156,37 @@
     flat[:, AT_CONV_TWO : AT_CONV_TWO + 9 * C] = eight(conv_b[...])
     for i in range(6):
         flat[:, AT_INNER + 384 * i : AT_INNER + 384 * i + C] = eight(squares[i][...])
+
+    own = [pl.ds(pl.multiple_of(BASES[i] + core * LENGTHS[i], 128), LENGTHS[i]) for i in range(OWN)]
+    for i in range(OWN):
+        w[i][core, x, z, yh] = flat[:, own[i]]
+    pl.semaphore_wait(barrier, 11 + jnp.where((chip == 0) | (chip == 3), 2, 0))
+
+    def send(src, dst, ss, rs, dev):
+        return pltpu.make_async_remote_copy(
+            src_ref=src, dst_ref=dst, send_sem=ss, recv_sem=rs, device_id=dev, device_id_type=MESH
+        )
+
+    pending = []
+
+    def go(copy):
+        copy.start()
+        pending.append(copy)
+        return copy
+
+    def crossing(i, k, to):
+        return send(flat.at[:, own[i]], w[i].at[core, x, z, yh], y_s.at[i, k], y_r.at[i], (mate, 2 * to + core))
+
+    for i in range(OWN):
+        for k in range(2):
+
+            @pl.when(chip == 0)
+            def _(i=i, k=k):
+                crossing(i, k, 3 - k).start()
+
+            @pl.when(chip == 3)
+            def _(i=i, k=k):
+                crossing(i, k, k).start()
 
     place = lax.broadcasted_iota(jnp.int32, (8, 128), 0) * 128 + lax.broadcasted_iota(jnp.int32, (8, 128), 1)
     root = math.sqrt(0.00085) + place.astype(F32) / (STEPS - 1) * (math.sqrt(0.012) - math.sqrt(0.00085))
@@ -173,37 +204,6 @@
     shifted = jnp.concatenate([west, noisy, east, jnp.zeros((4, OWN_TOKENS), F32)], axis=0).astype(BF16)
     nt[...] = shifted
     nview[s] = shifted
-    own = [pl.ds(pl.multiple_of(BASES[i] + core * LENGTHS[i], 128), LENGTHS[i]) for i in range(OWN)]
-    for i in range(OWN):
-        w[i][core, x, z, yh] = flat[:, own[i]]
-    pl.semaphore_wait(barrier, len(friends))
-
-    def send(src, dst, ss, rs, dev):
-        return pltpu.make_async_remote_copy(
-            src_ref=src, dst_ref=dst, send_sem=ss, recv_sem=rs, device_id=dev, device_id_type=MESH
-        )
-
-    pending = []
-
-    def go(copy):
-        copy.start()
-        pending.append(copy)
-        return copy
-
-    def crossing(i, k, to):
-        return send(flat.at[:, own[i]], w[i].at[core, x, z, yh], y_s.at[i, k], y_r.at[i], (mate, 2 * to + core))
-
-    for i in range(OWN):
-        for k in range(2):
-
-            @pl.when(chip == 0)
-            def _(i=i, k=k):
-                crossing(i, k, 3 - k).start()
-
-            @pl.when(chip == 3)
-            def _(i=i, k=k):
-                crossing(i, k, k).start()
-
     ns = []
     for d in range(1, 8):
         ns.append(go(send(nt, nview.at[s], n_s.at[d - 1], n_r.at[d - 1], (b, peers[d]))))
@@ -320,7 +320,9 @@
     nj = lax.broadcasted_iota(jnp.int32, (C, C), 1)
     apart = ni - lax.div(nj, 10) * 10
     gslim[...] = jnp.where((apart >= 0) & (apart < 10), 1.0, 0.0).astype(BF16)
-    vecs = jnp.concatenate([v[...] for v in held[15:20]] + [jnp.zeros((3, C), F32)], axis=0)
+    cross(2)
+    cross(3)
+    vecs = jnp.concatenate([v[...].reshape(1, C) for v in held[15:20]] + [jnp.zeros((3, C), F32)], axis=0)
     wide_vecs = exactly(mt, vecs, spread[...])
     taken = inlet[...].astype(F32)
     taken = [jnp.concatenate([taken[12 * q : 12 * q + 12], jnp.zeros((4, C), F32)], axis=0) for q in range(3)]
@@ -328,6 +330,8 @@
     win_wide = mt(win, spread[...]).astype(BF16)
     land(1, 0, 0)
     land(0, 0, 0)
+    land(3, 0, 0)
+    land(2, 0, 0)
 
     for copy in ns:
         copy.wait_recv()
@@ -342,10 +346,10 @@
 
     land(1, 0, 1)
     land(0, 0, 1)
+    land(2, 0, 1)
     land(0, 0, 2)
+    land(2, 0, 2)
     land(0, 0, 3)
-    cross(2)
-    cross(3)
 
     def start_sums(q, carry):
         total, squared = carry
@@ -382,27 +386,25 @@
                 taps[:, tap * C : (tap + 1) * C] = shifted[dy * ROW : dy * ROW + OWN_TOKENS]
 
     land(1, 1, 0)
-    land(2, 0, 0)
-    land(3, 0, 0)
+    land(3, 0, 1)
     taps[:, 9 * C :] = jnp.zeros((OWN_TOKENS, TAPS - 9 * C), BF16)
     factor, shift = affine(stacked(total, squared), gwide[...], wide_vecs[0:1], EPS_BLOCK)
     into_taps(start[...], factor, shift)
 
     land(1, 1, 1)
+    land(3, 1, 0)
     land(0, 1, 0)
-    land(2, 0, 1)
-    land(3, 0, 1)
+    land(2, 0, 3)
     row_p = lax.broadcasted_iota(jnp.int32, (C, 1), 0)
     target = 4 * row_p - 3 * lax.rem(row_p, 5)
     unit = lax.broadcasted_iota(jnp.int32, (C, 1280), 1)
     orders = [jnp.where(unit == target + 5 * i, 1.0, 0.0).astype(BF16) for i in range(4)]
-    bias_rows = jnp.broadcast_to(bias_a[...], (8, 1280))
+    bias_rows = jnp.broadcast_to(bias_a[...].reshape(1, 4 * C), (8, 4 * C))
     biases = [exactly(mt, exactly(mt, bias_rows, orders[i]), spread[...]) for i in range(4)]
-    land(2, 0, 2)
     land(1, 1, 2)
+    land(3, 1, 1)
     land(0, 1, 1)
     unpack(0)
-    land(2, 0, 3)
     land(1, 1, 3)
     unpack(1)
     waves = jnp.broadcast_to(wave[...], (8, C))
@@ -415,7 +417,8 @@
         part = silu(silu(inner + biases[i])).astype(BF16)
         hidden = hidden + mm(mm(part, spread[...]).astype(BF16), orders[i])
     embedded = mt(hidden.astype(BF16), wn[:, AT_SECOND : AT_SECOND + 1280])[0:1] + wide_vecs[4:5]
-    land(3, 1, 0)
+    land(3, 1, 2)
+    land(2, 1, 0)
     middle = (mt(taps[...], wn[:, AT_CONV_ONE : AT_CONV_ONE + TAPS]) + embedded).astype(BF16)
 
     def exchange(layer, field, edged):
@@ -483,15 +486,12 @@
         return gather_stats(layer, copies)
 
     swap = exchange(0, middle, mid6)
-    land(2, 1, 0)
-    land(3, 1, 1)
+    land(2, 1, 1)
+    unpack(2)
+    land(3, 1, 3)
     sums = exchanged(0, *swap)
     factor, shift = affine(sums, gwide[...], wide_vecs[1:2], EPS_BLOCK)
     into_taps(mid6[...], factor, shift)
-    land(3, 1, 2)
-    land(2, 1, 1)
-    unpack(2)
-    land(3, 1, 3)
     unpack(3)
     one = mt(taps[...], wn[:, AT_CONV_TWO : AT_CONV_TWO + TAPS])
     one = (one + start[ROW : ROW + OWN_TOKENS, :].astype(F32)).astype(BF16)
@@ -511,10 +511,6 @@
     def hop(source, towards, ss, rs):
         return send(nat.at[source], nat.at[source], ss, rs, (b, towards))
 
-    def kin(source_chip):
-        source = 2 * source_chip + core
-        return hop(source, sib, k_s.at[source_chip], k_r.at[source_chip])
-
     first_up = hop(s, lax.rem(s + 2, 8), up_s.at[0], up_r.at[0])
     first_dn = hop(s, lax.rem(s + 6, 8), dn_s.at[0], dn_r.at[0])
 
@@ -526,53 +522,30 @@
     def _():
         first_dn.start()
 
-    kin(chip).start()
-
-    def ups(h):
-        source = s - 2 * h
-        here = hop(source, lax.rem(s + 2, 8), up_s.at[min(h, 2)], up_r.at[h - 1])
-        on = hop(source, lax.rem(s + 2, 8), up_s.at[min(h, 2)], up_r.at[min(h, 2)])
-        return here, on
-
-    def dns(h):
-        source = s + 2 * h
-        here = hop(source, lax.rem(s + 6, 8), dn_s.at[min(h, 2)], dn_r.at[h - 1])
-        on = hop(source, lax.rem(s + 6, 8), dn_s.at[min(h, 2)], dn_r.at[min(h, 2)])
-        return here, on
-
-    for h in range(1, 4):
-
-        @pl.when(chip >= h)
-        def _(h=h):
-            here, on = ups(h)
-            here.wait_recv()
-            if h < 3:
-
-                @pl.when(chip < 3)
-                def _():
-                    on.start()
-
-            kin(chip - h).start()
-
-        @pl.when(chip + h <= 3)
-        def _(h=h):
-            here, on = dns(h)
-            here.wait_recv()
-            if h < 3:
-
-                @pl.when(chip > 0)
-                def _():
-                    on.start()
-
-            kin(chip + h).start()
-
-    for q in range(4):
-        source = 2 * q + 1 - core
-        hop(source, sib, k_s.at[q], k_r.at[q]).wait_recv()
-    sums = gather_stats(2, copies)
-    factor, shift = affine(sums[:, :C], gslim[...], third[...], EPS_GROUP)
+    def coming_up(h):
+        return hop(s - 2 * h, lax.rem(s + 2, 8), up_s.at[0], up_r.at[h - 1])
+
+    def going_up(h):
+        return hop(s - 2 * h, lax.rem(s + 2, 8), up_s.at[h], up_r.at[h])
+
+    def coming_dn(h):
+        return hop(s + 2 * h, lax.rem(s + 6, 8), dn_s.at[0], dn_r.at[h - 1])
+
+    def going_dn(h):
+        return hop(s + 2 * h, lax.rem(s + 6, 8), dn_s.at[h], dn_r.at[h])
+
     lane = lax.broadcasted_iota(jnp.int32, (1, WIDE), 1)
     real = lax.bitwise_and(lane, 7) < 5
+    sums = gather_stats(2, copies)
+    factor, shift = affine(sums[:, :C], gslim[...], third[...].reshape(1, C), EPS_GROUP)
+
+    def shares(q):
+        where = pl.ds(pl.multiple_of(q * 256, 256), 256)
+        at = lax.div(q, 2)
+        return (
+            send(keys.at[where], keys.at[where], k_s.at[at], k_r.at[at], (b, sib)),
+            send(values.at[where], values.at[where], k_s.at[4 + at], k_r.at[4 + at], (b, sib)),
+        )
 
     def tokens(q):
         normed = (nat[q].astype(F32) * factor + shift).astype(BF16)
@@ -585,17 +558,44 @@
         where = pl.ds(pl.multiple_of(q * 256, 256), 256)
         keys[where, :] = mt(inside, wn[:, AT_KEY : AT_KEY + C]).astype(BF16)
         values[where, :] = mt(inside, wn[:, AT_VALUE : AT_VALUE + C]).astype(BF16)
+        for copy in shares(q):
+            copy.start()
         return projected, inside
 
     projected, inside = tokens(s)
     base[...] = projected
     query[...] = mt(inside, wn[:, AT_QUERY : AT_QUERY + C]).astype(BF16)
-
-    def others(d, _):
-        tokens(lax.rem(s + d, 8))
-        return 0
-
-    lax.fori_loop(1, 8, others, 0)
+    for h in range(1, 4):
+
+        @pl.when(chip >= h)
+        def _(h=h):
+            coming_up(h).wait_recv()
+            if h < 3:
+
+                @pl.when(chip < 3)
+                def _():
+                    going_up(h).start()
+
+        @pl.when(chip + h <= 3)
+        def _(h=h):
+            coming_dn(h).wait_recv()
+            if h < 3:
+
+                @pl.when(chip > 0)
+                def _():
+                    going_dn(h).start()
+
+        @pl.when(chip >= h)
+        def _(h=h):
+            tokens(s - 2 * h)
+
+        @pl.when(chip + h <= 3)
+        def _(h=h):
+            tokens(s + 2 * h)
+
+    for q in range(4):
+        for copy in shares(2 * q + 1 - core):
+            copy.wait_recv()
 
     scale = math.log2(math.e) / math.sqrt(HEAD_SIZE)
     half = lax.broadcasted_iota(jnp.int32, (1, 128), 1) < 64
@@ -655,16 +655,17 @@
         first_dn.wait_send()
 
     for q in range(4):
-        kin(q).wait_send()
+        for copy in shares(2 * q + core):
+            copy.wait_send()
     for h in range(1, 3):
 
         @pl.when((chip >= h) & (chip < 3))
         def _(h=h):
-            ups(h)[1].wait_send()
+            going_up(h).wait_send()
 
         @pl.when((chip + h <= 3) & (chip > 0))
         def _(h=h):
-            dns(h)[1].wait_send()
+            going_dn(h).wait_send()
 
 
 def run_block(step, sources):
@@ -716,8 +717,8 @@
             dma((3,)),
             dma((3,)),
             dma((3,)),
-            dma((4,)),
-            dma((4,)),
+            dma((8,)),
+            dma((8,)),
         ],
         compiler_params=pltpu.CompilerParams(
             collective_id=0, has_side_effects=True, vmem_limit_bytes=58 << 20
@@ -769,9 +770,9 @@
         *(m.T for m in squares),
         inlet_conv,
         outlet_conv.T,
-        time_first_bias.reshape(1, 4 * C),
-        *(v.reshape(1, C) for v in vectors),
-        third_gain.reshape(1, C),
+        time_first_bias,
+        *vectors,
+        third_gain,
     ]
     result = run_block(timesteps, sources)
     return result.reshape(4, 4, ROW).transpose(1, 2, 0)[None]

time: 137 us -> 117 us (0.85)
  Pallas kernels: 128 us -> 112 us
  local copies, waits for them, and re-layouts: 6.94 us -> 2.84 us
    pallas_call x1, Pallas kernels: 128 us -> 112 us  [run_block(): pl.pallas_call(block_kernel, out_shape=jax.ShapeDtypeStruct((4, OWN_TOKEN...]
    reshape x7 -> x0, local copies, waits for them, and re-layouts: 4.01 us -> none  [the longest x5 2.82 us: body(): v.reshape(1, C)]
where the time goes in v4:
time: 117 us
  Pallas kernels  112 us (96%)
  local copies, waits for them, and re-layouts  2.84 us (2%)
  other arithmetic  1.32 us (1%)
    pallas_call x1, Pallas kernels, run_block(): pl.pallas_call(block_kernel, out_shape=jax.ShapeDtypeStruct((4, OWN_TOKEN...  112 us

profile of v4, /device:TPU:1, one launch (start us, length us, event | category | flops | bytes accessed | tf_op | source)
XLA Modules:
  0.0 116.6 jit_solution(2257816557669834062)
XLA Ops:
  0.7 0.7 copy.24
  1.4 0.0 copy-start
  1.4 0.1 reshape.36
  1.4 0.6 copy-done
  2.1 0.1 reshape.35
  2.1 0.6 pad_maximum_fusion.refs_0_
  2.7 0.1 fusion
  2.8 0.6 pad_maximum_fusion.1.refs_1_
  3.5 111.8 %unet_level.1 = f32[4,256]{1,0:T(4,128)} custom-call(s32[1]{0:T(128)S(6)} %copy.28.step, f32[8,256]{1,0:T(8,128)} %pad_maximum_fusion.refs_0_, f32[1,320]{1,0:T(1,128)} %pad_maximum_fusion.1.refs_1_, bf16[20,320]{1,0:T(8,128)(2,1)} %bitcast.27, bf16[5,1280]{1,0:T(8,128)(2,1)} %bitcast.26, bf16[5,2880]{1,0:T(8,128)(2,1)} %bitcast.23, ...), custom_call_target="tpu_custom_call" | custom-call | tf_op jit(solution)/shard_map/unet_level/pallas_call | solution.py:674
  115.2 0.8 reshape.37
  116.0 0.6 copy.27
  (1 shorter events, 0.0 us)
Async XLA Ops:
  1.4 0.7 copy-start

commit v5 on v4

--- a/solution.py
+++ b/solution.py
@@ -68,6 +68,12 @@
         w1,
         w2,
         w3,
+        d0,
+        d1,
+        d2,
+        d3,
+        orders,
+        pack,
         wn,
         flat,
         taps,
@@ -110,6 +116,7 @@
         k_r,
     ) = refs[43:]
     w = (w0, w1, w2, w3)
+    dense = (d0, d1, d2, d3)
     b = lax.axis_index("batch")
     s = lax.axis_index("space")
     yh = lax.rem(b, 2)
@@ -160,34 +167,6 @@
     own = [pl.ds(pl.multiple_of(BASES[i] + core * LENGTHS[i], 128), LENGTHS[i]) for i in range(OWN)]
     for i in range(OWN):
         w[i][core, x, z, yh] = flat[:, own[i]]
-    pl.semaphore_wait(barrier, 11 + jnp.where((chip == 0) | (chip == 3), 2, 0))
-
-    def send(src, dst, ss, rs, dev):
-        return pltpu.make_async_remote_copy(
-            src_ref=src, dst_ref=dst, send_sem=ss, recv_sem=rs, device_id=dev, device_id_type=MESH
-        )
-
-    pending = []
-
-    def go(copy):
-        copy.start()
-        pending.append(copy)
-        return copy
-
-    def crossing(i, k, to):
-        return send(flat.at[:, own[i]], w[i].at[core, x, z, yh], y_s.at[i, k], y_r.at[i], (mate, 2 * to + core))
-
-    for i in range(OWN):
-        for k in range(2):
-
-            @pl.when(chip == 0)
-            def _(i=i, k=k):
-                crossing(i, k, 3 - k).start()
-
-            @pl.when(chip == 3)
-            def _(i=i, k=k):
-                crossing(i, k, k).start()
-
     place = lax.broadcasted_iota(jnp.int32, (8, 128), 0) * 128 + lax.broadcasted_iota(jnp.int32, (8, 128), 1)
     root = math.sqrt(0.00085) + place.astype(F32) / (STEPS - 1) * (math.sqrt(0.012) - math.sqrt(0.00085))
     abar = jnp.where(place <= step[0], 1.0 - root * root, 1.0)
@@ -204,6 +183,65 @@
     shifted = jnp.concatenate([west, noisy, east, jnp.zeros((4, OWN_TOKENS), F32)], axis=0).astype(BF16)
     nt[...] = shifted
     nview[s] = shifted
+    wide_i = lax.broadcasted_iota(jnp.int32, (WIDE, C), 0)
+    slim_j = lax.broadcasted_iota(jnp.int32, (WIDE, C), 1)
+    hit = (lax.shift_right_logical(wide_i, 3) * 5 + lax.bitwise_and(wide_i, 7) == slim_j) & (
+        lax.bitwise_and(wide_i, 7) < 5
+    )
+    spread[...] = jnp.where(hit, 1.0, 0.0).astype(BF16)
+    gi = lax.broadcasted_iota(jnp.int32, (WIDE, WIDE), 0)
+    gj = lax.broadcasted_iota(jnp.int32, (WIDE, WIDE), 1)
+    same = lax.shift_right_logical(gi, 4) == lax.shift_right_logical(gj, 4)
+    gwide[...] = jnp.where(same, 1.0, 0.0).astype(BF16)
+    ni = lax.broadcasted_iota(jnp.int32, (C, C), 0)
+    nj = lax.broadcasted_iota(jnp.int32, (C, C), 1)
+    apart = ni - lax.div(nj, 10) * 10
+    gslim[...] = jnp.where((apart >= 0) & (apart < 10), 1.0, 0.0).astype(BF16)
+    pr = lax.broadcasted_iota(jnp.int32, (80, 128), 0)
+    pc = lax.broadcasted_iota(jnp.int32, (80, 128), 1)
+    hit = (lax.shift_right_logical(pc, 3) * 5 + lax.bitwise_and(pc, 7) == pr) & (lax.bitwise_and(pc, 7) < 5)
+    pack[...] = jnp.where(hit, 1.0, 0.0).astype(BF16)
+    vecs = jnp.concatenate([v[...].reshape(1, C) for v in held[15:20]] + [jnp.zeros((3, C), F32)], axis=0)
+    wide_vecs = exactly(mt, vecs, spread[...])
+    taken = inlet[...].astype(F32)
+    taken = [jnp.concatenate([taken[12 * q : 12 * q + 12], jnp.zeros((4, C), F32)], axis=0) for q in range(3)]
+    win = jnp.concatenate(taken + [jnp.zeros((80, C), F32)], axis=0).astype(BF16)
+    win_wide = mt(win, spread[...]).astype(BF16)
+    row_p = lax.broadcasted_iota(jnp.int32, (C, 1), 0)
+    target = 4 * row_p - 3 * lax.rem(row_p, 5)
+    unit = lax.broadcasted_iota(jnp.int32, (C, 1280), 1)
+    for i in range(4):
+        orders[i] = jnp.where(unit == target + 5 * i, 1.0, 0.0).astype(BF16)
+    bias_rows = jnp.broadcast_to(bias_a[...].reshape(1, 4 * C), (8, 4 * C))
+    biases = [exactly(mt, exactly(mt, bias_rows, orders[i]), spread[...]) for i in range(4)]
+    pl.semaphore_wait(barrier, 11 + jnp.where((chip == 0) | (chip == 3), 2, 0))
+
+    def send(src, dst, ss, rs, dev):
+        return pltpu.make_async_remote_copy(
+            src_ref=src, dst_ref=dst, send_sem=ss, recv_sem=rs, device_id=dev, device_id_type=MESH
+        )
+
+    pending = []
+
+    def go(copy):
+        copy.start()
+        pending.append(copy)
+        return copy
+
+    def crossing(i, k, to):
+        return send(flat.at[:, own[i]], w[i].at[core, x, z, yh], y_s.at[i, k], y_r.at[i], (mate, 2 * to + core))
+
+    for i in range(OWN):
+        for k in range(2):
+
+            @pl.when(chip == 0)
+            def _(i=i, k=k):
+                crossing(i, k, 3 - k).start()
+
+            @pl.when(chip == 3)
+            def _(i=i, k=k):
+                crossing(i, k, k).start()
+
     ns = []
     for d in range(1, 8):
         ns.append(go(send(nt, nview.at[s], n_s.at[d - 1], n_r.at[d - 1], (b, peers[d]))))
@@ -252,14 +290,16 @@
 
     def rings(i, k):
         wk = w[i].at[k]
+        dk = dense[i].at[k]
+        cuts = (pl.ds(0, 640), pl.ds(640, LENGTHS[i] - 640))
         if i % 2 == 0:
             small = z_ring(i, lambda q: wk.at[x, q], lambda q, h: wk.at[x, q, h])
-            large = x_ring(i, lambda q: wk.at[q], lambda q, h: wk.at[q, pl.ds(4 * h, 4)])
-            mine = wk.at[x]
+            large = x_ring(i, lambda q: dk.at[q], lambda q, h: dk.at[q, :, cuts[h]])
+            mine = dk.at[x]
         else:
             small = x_ring(i, lambda q: wk.at[q, z], lambda q, h: wk.at[q, z, h])
-            large = z_ring(i, lambda q: wk.at[:, q], lambda q, h: wk.at[pl.ds(2 * h, 2), q])
-            mine = wk.at[:, z]
+            large = z_ring(i, lambda q: dk.at[q], lambda q, h: dk.at[q, :, cuts[h]])
+            mine = dk.at[z]
         return small, large, mine
 
     mine_rings = [rings(i, core) for i in range(OWN)]
@@ -279,6 +319,12 @@
         if t + 1 < count:
             launch(i, which, t + 1)
         elif which == 0:
+            if i % 2 == 0:
+                rows = w[i][core, x].astype(F32).reshape(128, LENGTHS[i]).astype(BF16)
+                dense[i][core, x] = mm(pack[...], rows).astype(BF16)
+            else:
+                rows = w[i][core, :, z].astype(F32).reshape(64, LENGTHS[i]).astype(BF16)
+                dense[i][core, z] = mm(pack[0:40, 0:64], rows).astype(BF16)
             launch(i, 1, 0)
             to_sib(i, 0, mine_rings[i][2])
         if which == 1:
@@ -295,39 +341,27 @@
         for j, ref in enumerate(refs):
             send(ref, ref, c_s.at[i, j], c_r.at[i, j], (b, sib)).wait_recv()
 
-        def two(p, _):
+        grow = pack[...].astype(F32).T.astype(BF16)
+
+        def wide_rows(q, _):
             for k in range(2):
-                both = w[i][k, lax.div(p, 8), lax.rem(p, 8)].astype(F32).reshape(16, LENGTHS[i])
                 at = BASES[i] + k * LENGTHS[i]
-                wn[pl.ds(pl.multiple_of(p * 16, 16), 16), at : at + LENGTHS[i]] = both.astype(BF16)
+                lanes = slice(at, at + LENGTHS[i])
+                if i % 2 == 0:
+                    rows = mm(grow, dense[i][k, q]).astype(BF16)
+                    wn[pl.ds(pl.multiple_of(q * 128, 128), 128), lanes] = rows
+                else:
+                    rows = mm(grow[0:64, 0:40], dense[i][k, q]).astype(BF16)
+                    for xx in range(4):
+                        wn[pl.ds(pl.multiple_of(128 * xx + q * 16, 16), 16), lanes] = rows[16 * xx : 16 * xx + 16]
             return 0
 
-        lax.fori_loop(0, 32, two, 0)
-
-    wide_i = lax.broadcasted_iota(jnp.int32, (WIDE, C), 0)
-    slim_j = lax.broadcasted_iota(jnp.int32, (WIDE, C), 1)
-    hit = (lax.shift_right_logical(wide_i, 3) * 5 + lax.bitwise_and(wide_i, 7) == slim_j) & (
-        lax.bitwise_and(wide_i, 7) < 5
-    )
-    spread[...] = jnp.where(hit, 1.0, 0.0).astype(BF16)
+        lax.fori_loop(0, 8 if i % 2 else 4, wide_rows, 0)
+
     cross(0)
     cross(1)
-    gi = lax.broadcasted_iota(jnp.int32, (WIDE, WIDE), 0)
-    gj = lax.broadcasted_iota(jnp.int32, (WIDE, WIDE), 1)
-    same = lax.shift_right_logical(gi, 4) == lax.shift_right_logical(gj, 4)
-    gwide[...] = jnp.where(same, 1.0, 0.0).astype(BF16)
-    ni = lax.broadcasted_iota(jnp.int32, (C, C), 0)
-    nj = lax.broadcasted_iota(jnp.int32, (C, C), 1)
-    apart = ni - lax.div(nj, 10) * 10
-    gslim[...] = jnp.where((apart >= 0) & (apart < 10), 1.0, 0.0).astype(BF16)
     cross(2)
     cross(3)
-    vecs = jnp.concatenate([v[...].reshape(1, C) for v in held[15:20]] + [jnp.zeros((3, C), F32)], axis=0)
-    wide_vecs = exactly(mt, vecs, spread[...])
-    taken = inlet[...].astype(F32)
-    taken = [jnp.concatenate([taken[12 * q : 12 * q + 12], jnp.zeros((4, C), F32)], axis=0) for q in range(3)]
-    win = jnp.concatenate(taken + [jnp.zeros((80, C), F32)], axis=0).astype(BF16)
-    win_wide = mt(win, spread[...]).astype(BF16)
     land(1, 0, 0)
     land(0, 0, 0)
     land(3, 0, 0)
@@ -395,18 +429,10 @@
     land(3, 1, 0)
     land(0, 1, 0)
     land(2, 0, 3)
-    row_p = lax.broadcasted_iota(jnp.int32, (C, 1), 0)
-    target = 4 * row_p - 3 * lax.rem(row_p, 5)
-    unit = lax.broadcasted_iota(jnp.int32, (C, 1280), 1)
-    orders = [jnp.where(unit == target + 5 * i, 1.0, 0.0).astype(BF16) for i in range(4)]
-    bias_rows = jnp.broadcast_to(bias_a[...].reshape(1, 4 * C), (8, 4 * C))
-    biases = [exactly(mt, exactly(mt, bias_rows, orders[i]), spread[...]) for i in range(4)]
     land(1, 1, 2)
     land(3, 1, 1)
     land(0, 1, 1)
     unpack(0)
-    land(1, 1, 3)
-    unpack(1)
     waves = jnp.broadcast_to(wave[...], (8, C))
     hidden = jnp.zeros((8, 1280), F32)
     for i in range(4):
@@ -417,6 +443,8 @@
         part = silu(silu(inner + biases[i])).astype(BF16)
         hidden = hidden + mm(mm(part, spread[...]).astype(BF16), orders[i])
     embedded = mt(hidden.astype(BF16), wn[:, AT_SECOND : AT_SECOND + 1280])[0:1] + wide_vecs[4:5]
+    land(1, 1, 3)
+    unpack(1)
     land(3, 1, 2)
     land(2, 1, 0)
     middle = (mt(taps[...], wn[:, AT_CONV_ONE : AT_CONV_ONE + TAPS]) + embedded).astype(BF16)
@@ -678,6 +706,8 @@
         out_specs=pl.BlockSpec(memory_space=pltpu.VMEM),
         scratch_shapes=[pltpu.VMEM(a.shape, a.dtype) for a in sources]
         + [pltpu.VMEM((2, 4, 8, 2, 8, length), BF16) for length in LENGTHS]
+        + [pltpu.VMEM((2, 8, 40, n) if i % 2 else (2, 4, 80, n), BF16) for i, n in enumerate(LENGTHS)]
+        + [pltpu.VMEM((4, C, 4 * C), BF16), pltpu.VMEM((80, 128), BF16)]
         + [
             pltpu.VMEM((WIDE, LANES), BF16),
             pltpu.VMEM((8, LANES), BF16),

time: 117 us -> 115 us (0.983)
  Pallas kernels: 112 us -> 109 us
    pallas_call x1, Pallas kernels: 112 us -> 109 us  [run_block(): pl.pallas_call(block_kernel, out_shape=jax.ShapeDtypeStruct((4, OWN_TOKEN...]
where the time goes in v5:
time: 115 us; the launch traced here: 114 us
  Pallas kernels  109 us (95%)
  local copies, waits for them, and re-layouts  2.84 us (2%)
  other arithmetic  1.32 us (1%)
    pallas_call x1, Pallas kernels, run_block(): pl.pallas_call(block_kernel, out_shape=jax.ShapeDtypeStruct((4, OWN_TOKEN...  109 us

profile of v5, /device:TPU:1, one launch (start us, length us, event | category | flops | bytes accessed | tf_op | source)
XLA Modules:
  0.0 114.2 jit_solution(2050016097783699089)
XLA Ops:
  0.7 0.7 copy.24
  1.4 0.0 copy-start
  1.4 0.1 reshape.36
  1.4 0.6 copy-done
  2.1 0.1 reshape.35
  2.1 0.6 pad_maximum_fusion.refs_0_
  2.7 0.1 fusion
  2.8 0.6 pad_maximum_fusion.1.refs_1_
  3.5 109.4 %unet_level.1 = f32[4,256]{1,0:T(4,128)} custom-call(s32[1]{0:T(128)S(6)} %copy.28.step, f32[8,256]{1,0:T(8,128)} %pad_maximum_fusion.refs_0_, f32[1,320]{1,0:T(1,128)} %pad_maximum_fusion.1.refs_1_, bf16[20,320]{1,0:T(8,128)(2,1)} %bitcast.27, bf16[5,1280]{1,0:T(8,128)(2,1)} %bitcast.26, bf16[5,2880]{1,0:T(8,128)(2,1)} %bitcast.23, ...), custom_call_target="tpu_custom_call" | custom-call | tf_op jit(solution)/shard_map/unet_level/pallas_call | solution.py:702
  112.8 0.8 reshape.37
  113.6 0.6 copy.27
  (1 shorter events, 0.0 us)
Async XLA Ops:
  1.4 0.7 copy-start
